TPU v7x, 32 devices: a whole 2x2x4 slice. The times are simulated.
32 devices in a mesh: view: 4 (over x, core), pencil: 8 (over z, y).
Axes of the slice: x: 2, y: 2, z: 4, core: 2. Of those that a mesh axis runs over, the one named last changes fastest.
Arguments:
- recorded: float32 [4, 256, 256, 256], P('view', 'pencil'), may hold values from 0.5 to 4
- spectral_weight: float32 [4, 256, 256, 256], P('view', None, 'pencil'), may hold values from 0.05 to 1
- psf_taps: float32 [4, 3, 9], replicated, may hold values from 0.1 to 1
Outputs:
- joined_volume: float32 [256, 256, 256], P('pencil', 'view')
- estimate: float32 [256, 256, 256], P('pencil', 'view')
All inputs are finite; a program needn't handle non-finite values.
Results may differ from a plain program's by a relative error of at most 0.00029.
Values sent between devices are 32-bit elements; how exact they have to be, the bound alone decides.
A program may use at most 192 MiB of HBM per device.

v0:
```python
import math

import jax
import jax.numpy as jnp
from jax import lax
from jax.sharding import PartitionSpec as P

ITERS = 2
CHUNKS = 2


def padded_2(shard, sides, width):
    for axis, dim in sides:
        devices, length = (lax.axis_size(axis), shard.shape[dim])
        up = [(i, (i + 1) % devices) for i in range(devices - 1)]
        down = [(j, i) for i, j in up]
        last = lax.slice_in_dim(shard, length - width, length, axis=dim)
        leading = lax.slice_in_dim(shard, 0, width, axis=dim)
        before = lax.ppermute(last, axis, up)
        after = lax.ppermute(leading, axis, down)
        shard = jnp.concatenate([before, shard, after], axis=dim)
    return shard


def tables(length):
    positions = jnp.arange(length, dtype=jnp.int32)
    product = positions[:, None] * positions[None, :] % length
    phases = product.astype(jnp.float32) * (2.0 * math.pi / length)
    return (jnp.cos(phases), jnp.sin(phases))


def mix(form, left, right):
    return jnp.einsum(form, left, right, precision=lax.Precision.HIGH)


def folded(full, axis, dim, width):
    devices, length = (lax.axis_size(axis), full.shape[dim] - 2 * width)
    up = [(i, (i + 1) % devices) for i in range(devices - 1)]
    down = [(j, i) for i, j in up]
    before = lax.slice_in_dim(full, 0, width, axis=dim)
    after = lax.slice_in_dim(full, length + width, length + 2 * width, axis=dim)
    own = lax.slice_in_dim(full, width, length + width, axis=dim)
    from_below = lax.ppermute(after, axis, up)
    from_above = lax.ppermute(before, axis, down)
    spread = [(0, 0, 0)] * full.ndim
    spread[dim] = (0, length - width, 0)
    lower = lax.pad(from_below, jnp.float32(0), spread)
    spread[dim] = (length - width, 0, 0)
    return own + lower + lax.pad(from_above, jnp.float32(0), spread)


def band(taps, rows, columns, shift):
    offset = jnp.arange(columns)[None, :] - jnp.arange(rows)[:, None] + shift
    total = jnp.zeros((taps.shape[0], rows, columns), jnp.float32)
    for t in range(taps.shape[1]):
        total = total + jnp.where(offset == t, taps[:, t, None, None], 0.0)
    return total


def joined_of(slab, weights):
    view_count, view_index = lax.axis_size("view"), lax.axis_index("view")
    nx, ny = slab.shape[2], slab.shape[1]
    cos_x, sin_x = tables(nx)
    cos_y, sin_y = tables(ny)
    width = nx // CHUNKS
    sent = []
    for chunk in range(CHUNKS):
        part = slice(chunk * width, (chunk + 1) * width)
        real = mix("zyx,xk->zyk", slab, cos_x[:, part])
        imag = -mix("zyx,xk->zyk", slab, sin_x[:, part])
        out_real = mix("zyx,yk->zkx", real, cos_y) + mix("zyx,yk->zkx", imag, sin_y)
        out_imag = mix("zyx,yk->zkx", imag, cos_y) - mix("zyx,yk->zkx", real, sin_y)
        sent.append([
            lax.all_to_all(piece, "pencil", split_axis=1, concat_axis=0, tiled=True)
            for piece in (out_real, out_imag)
        ])
    inverse = []
    for chunk in range(CHUNKS):
        real, imag = sent[chunk]
        nz = real.shape[0]
        cos_z, sin_z = tables(nz)
        weight = weights[:, :, chunk * width:(chunk + 1) * width]
        out_real = weight * (mix("zyx,zk->kyx", real, cos_z) + mix("zyx,zk->kyx", imag, sin_z))
        out_imag = weight * (mix("zyx,zk->kyx", imag, cos_z) - mix("zyx,zk->kyx", real, sin_z))
        real = lax.psum_scatter(out_real, "view", scatter_dimension=1, tiled=True)
        imag = lax.psum_scatter(out_imag, "view", scatter_dimension=1, tiled=True)
        inverse.append((
            mix("kyx,kz->zyx", real, cos_z) - mix("kyx,kz->zyx", imag, sin_z),
            mix("kyx,kz->zyx", real, sin_z) + mix("kyx,kz->zyx", imag, cos_z),
        ))
    real = jnp.concatenate([pair[0] for pair in inverse], axis=2)
    imag = jnp.concatenate([pair[1] for pair in inverse], axis=2)
    rows = real.shape[1]
    moved = [
        lax.all_to_all(piece, "pencil", split_axis=0, concat_axis=1, tiled=True)
        for piece in (
            mix("zyk,kx->zyx", real, cos_x) - mix("zyk,kx->zyx", imag, sin_x),
            mix("zyk,kx->zyx", real, sin_x) + mix("zyk,kx->zyx", imag, cos_x),
        )
    ]
    scale = 1.0 / float(nz * ny * nx)
    held = [
        lax.dynamic_index_in_dim(
            table.reshape(-1, view_count, rows, ny), view_index, 1, keepdims=False
        ).reshape(-1, ny) * scale
        for table in (cos_y, sin_y)
    ]
    partial = mix("zkx,ky->zyx", moved[0], held[0]) - mix("zkx,ky->zyx", moved[1], held[1])
    return lax.psum_scatter(partial, "view", scatter_dimension=1, tiled=True)


def body(recorded, spectral_weight, psf_taps):
    view_count = lax.axis_size("view")
    joined_volume = joined_of(recorded[0], spectral_weight[0])
    kernels = psf_taps / jnp.sum(psf_taps, axis=-1, keepdims=True)
    margin = kernels.shape[-1] // 2
    stacked = lax.all_to_all(recorded, "view", split_axis=2, concat_axis=0, tiled=True)
    depth, rows, length = joined_volume.shape
    views = kernels.shape[0]
    blur_z = band(kernels[:, 0], depth, depth + 2 * margin, 0)
    blur_y = band(kernels[:, 1], rows, rows + 2 * margin, 0)
    blur_x = band(kernels[:, 2], length, length, margin)
    local = 0.1 + jax.nn.softplus(joined_volume)
    for repeat in range(ITERS):
        padded = padded_2(local, (("view", 1), ("pencil", 0)), margin)
        field = mix("vza,abx->vzbx", blur_z, padded)
        field = mix("vyb,vzbx->vzyx", blur_y, field)
        ratio = stacked / mix("vzyx,vcx->vzyc", field, blur_x)
        field = mix("vzyc,vcx->vzyx", ratio, blur_x)
        field = mix("vyb,vzyx->vzbx", blur_y, field)
        total = mix("vza,vzbx->abx", blur_z, field)
        total = folded(folded(total, "pencil", 0, margin), "view", 1, margin)
        local = local * total / view_count
    return (joined_volume, local)


def solution(mesh):
    return jax.shard_map(
        body,
        mesh=mesh,
        in_specs=(P("view", "pencil", None, None), P("view", None, "pencil", None), P()),
        out_specs=(P("pencil", "view", None), P("pencil", "view", None)),
        check_vma=False,
    )
```

profile of v0, /device:TPU:25, one launch (start us, length us, event | category | flops | bytes accessed | tf_op | source)
XLA Modules:
  0.0 1051.3 jit_solution(16029238604463743606)
XLA Ops:
  9.1 8.0 fusion.12
  53.4 79.3 %all-to-all-done = f32[32,256,128]{2,0,1:T(8,128)} async-done(((f32[32,256,128]{2,0,1:T(8,128)}), f32[32,256,128]{2,0,1:T(8,128)}, u32[]{:S(2)}, u32[]{:S(2)}) %all-to-all-start) | async-done | bytes 4194336 | tf_op jit(solution)/shard_map/all_to_all | solution.py:74
  137.8 11.7 %copy.275 = f32[1,256,32,256]{3,1,2,0:T(8,128)} copy(f32[1,256,32,256]{3,2,1,0:T(8,128)} %param.4) | data formatting | bytes 16777216 | tf_op args[1]
  179.4 50.5 %all-to-all-done.1 = f32[32,256,128]{2,0,1:T(8,128)} async-done(((f32[32,256,128]{2,0,1:T(8,128)}), f32[32,256,128]{2,0,1:T(8,128)}, u32[]{:S(2)}, u32[]{:S(2)}) %all-to-all-start.1) | async-done | bytes 4194336 | tf_op jit(solution)/shard_map/all_to_all | solution.py:74
  242.5 8.6 subtract_bitcast_fusion.1
  278.4 74.2 %all-to-all-done.3 = f32[32,256,128]{2,0,1:T(8,128)} async-done(((f32[32,256,128]{2,0,1:T(8,128)}), f32[32,256,128]{2,0,1:T(8,128)}, u32[]{:S(2)}, u32[]{:S(2)}) %all-to-all-start.3) | async-done | bytes 4194336 | tf_op jit(solution)/shard_map/all_to_all | solution.py:74
  357.3 9.0 subtract_multiply_fusion.1
  371.2 78.6 %all-to-all-done.2 = f32[32,256,128]{2,0,1:T(8,128)} async-done(((f32[32,256,128]{2,0,1:T(8,128)}), f32[32,256,128]{2,0,1:T(8,128)}, u32[]{:S(2)}, u32[]{:S(2)}) %all-to-all-start.2) | async-done | bytes 4194336 | tf_op jit(solution)/shard_map/all_to_all | solution.py:74
  468.8 8.5 add_multiply_fusion
  480.5 27.2 %reduce-scatter.12.cloned.1.call-done = f32[256,8,128]{2,0,1:T(8,128)} async-done(((f32[256,32,128]{2,0,1:T(8,128)}), f32[256,8,128]{2,0,1:T(8,128)}) %reduce-scatter.12.cloned.1.call-update) | async-done | bytes 1048592 | tf_op jit(solution)/shard_map/reduce_scatter | solution.py:86
  524.6 30.1 %reduce-scatter.10.cloned.1.call-done = f32[256,8,128]{2,0,1:T(8,128)} async-done(((f32[256,32,128]{2,0,1:T(8,128)}), f32[256,8,128]{2,0,1:T(8,128)}) %reduce-scatter.10.cloned.1.call-update) | async-done | bytes 1048592 | tf_op jit(solution)/shard_map/reduce_scatter | solution.py:85
  582.3 39.7 %all-to-all-done.4 = f32[256,8,256]{2,1,0:T(8,128)} async-done(((f32[256,8,256]{2,1,0:T(8,128)}), f32[256,8,256]{2,1,0:T(8,128)}, u32[]{:S(2)}, u32[]{:S(2)}) %all-to-all-start.4) | async-done | bytes 2097184 | tf_op jit(solution)/shard_map/all_to_all | solution.py:95
  634.9 39.3 %all-to-all-done.5 = f32[256,8,256]{2,1,0:T(8,128)S(1)} async-done(((f32[256,8,256]{2,1,0:T(8,128)}), f32[256,8,256]{2,1,0:T(8,128)S(1)}, u32[]{:S(2)}, u32[]{:S(2)}) %all-to-all-start.5) | async-done | bytes 2097184 | tf_op jit(solution)/shard_map/all_to_all | solution.py:95
  674.1 8.5 subtract_bitcast_fusion
  682.6 13.5 %copy.158 = f32[1,32,256,256]{3,1,0,2:T(8,128)} copy(f32[1,32,256,256]{3,2,1,0:T(8,128)} %param.3) | data formatting | bytes 16777216 | tf_op args[0]
  707.1 91.0 %reduce-scatter.14.cloned.1.call-done = f32[32,64,256]{2,1,0:T(8,128)} async-done(((f32[32,256,256]{2,1,0:T(8,128)}), f32[32,64,256]{2,1,0:T(8,128)}) %reduce-scatter.14.cloned.1.call-update) | async-done | bytes 2097168 | tf_op jit(solution)/shard_map/reduce_scatter | solution.py:109
  808.5 30.7 %collective-permute-done = f32[32,4,256]{2,1,0:T(4,128)S(1)} collective-permute-done((f32[32,4,256]{2,1,0:T(4,128)S(1)}, f32[32,4,256]{2,1,0:T(4,128)S(1)}, u32[]{:S(2)}, u32[]{:S(2)}) %collective-permute-start) | collective-permute-done | bytes 131104 | tf_op jit(solution)/shard_map/ppermute | solution.py:19
  852.5 11.5 %copy.159 = f32[1,32,256,256]{3,2,1,0:T(8,128)} copy(f32[1,32,256,256]{3,1,0,2:T(8,128)} %all-to-all-done.6) | data formatting | bytes 16777216 | tf_op jit(solution)/shard_map/all_to_all | solution.py:117
  870.2 10.8 %fusion.44 = f32[4,32,64,256]{3,2,1,0:T(8,128)} fusion(f32[4,32,72,256]{3,1,2,0:T(8,128)S(1)} %fusion.52, f32[4]{0:T(128)S(1)} %copy-done.66, f32[4]{0:T(128)S(1)} %copy-done.67, f32[4]{0:T(128)S(1)} %copy-done.68, f32[4]{0:T(128)S(1)} %copy-done.69, f32[4]{0:T(128)S(1)} %copy-done.70, f32[4]{0:T(128)S(1)} %copy-done.71, f32[4]{0:T(128)S(1)} %copy-done.72, ...), kind=kOutput, calls=%fused_computation.57 | convolution fusion | flops 906283008 | bytes 17867408 | tf_op jit(solution)/shard_map/vyb,vzbx->vzyx/dot_general | solution.py:33
  881.1 12.1 %fusion.56 = f32[4,32,64,256]{3,2,0,1:T(8,128)} fusion(f32[4,32,64,256]{3,2,0,1:T(8,128)S(1)} %bitcast.273, f32[4,32,64,256]{3,2,1,0:T(8,128)} %fusion.44, f32[4]{0:T(128)S(1)} %copy-done.75, f32[4]{0:T(128)S(1)} %copy-done.76, f32[4]{0:T(128)S(1)} %copy-done.77, f32[4]{0:T(128)S(1)} %copy-done.78, f32[4]{0:T(128)S(1)} %copy-done.79, f32[4]{0:T(128)S(1)} %copy-done.80, ...), kind=kOutput, calls=%fused_computation.67 | convolution fusion | flops 3227779072 | bytes 25755792 | tf_op jit(solution)/shard_map/vzyx,vcx->vzyc/dot_general | solution.py:33
  893.2 8.2 fusion.20
  965.9 10.7 %fusion.47 = f32[4,32,64,256]{3,2,1,0:T(8,128)} fusion(f32[4,32,72,256]{3,1,2,0:T(8,128)S(1)} %fusion.50, f32[4]{0:T(128)S(1)} %copy-done.66, f32[4]{0:T(128)S(1)} %copy-done.67, f32[4]{0:T(128)S(1)} %copy-done.68, f32[4]{0:T(128)S(1)} %copy-done.69, f32[4]{0:T(128)S(1)} %copy-done.70, f32[4]{0:T(128)S(1)} %copy-done.71, f32[4]{0:T(128)S(1)} %copy-done.72, ...), kind=kOutput, calls=%fused_computation.58 | convolution fusion | flops 906283008 | bytes 17867408 | tf_op jit(solution)/shard_map/vyb,vzbx->vzyx/dot_general | solution.py:33
  976.7 13.9 %fusion.59 = f32[4,32,64,256]{3,2,0,1:T(8,128)} fusion(f32[4,32,64,256]{3,2,0,1:T(8,128)} %bitcast.270, f32[4,32,64,256]{3,2,1,0:T(8,128)} %fusion.47, f32[4]{0:T(128)S(1)} %copy-done.75, f32[4]{0:T(128)S(1)} %copy-done.76, f32[4]{0:T(128)S(1)} %copy-done.77, f32[4]{0:T(128)S(1)} %copy-done.78, f32[4]{0:T(128)S(1)} %copy-done.79, f32[4]{0:T(128)S(1)} %copy-done.80, ...), kind=kOutput, calls=%fused_computation.68 | convolution fusion | flops 3227779072 | bytes 25755792 | tf_op jit(solution)/shard_map/vzyx,vcx->vzyc/dot_general | solution.py:33
  990.6 11.2 %fusion.16 = f32[4,32,64,256]{3,2,1,0:T(8,128)} fusion(f32[4,32,64,256]{3,2,0,1:T(8,128)} %fusion.59, f32[4]{0:T(128)S(1)} %copy-done.75, f32[4]{0:T(128)S(1)} %copy-done.76, f32[4]{0:T(128)S(1)} %copy-done.77, f32[4]{0:T(128)S(1)} %copy-done.78, f32[4]{0:T(128)S(1)} %copy-done.79, f32[4]{0:T(128)S(1)} %copy-done.80, f32[4]{0:T(128)S(1)} %copy-done.81, ...), kind=kOutput, calls=%fused_computation.16 | convolution fusion | flops 3225681920 | bytes 17367184 | tf_op jit(solution)/shard_map/vzyc,vcx->vzyx/dot_general | solution.py:33
  (348 shorter events, 348.3 us)
Async XLA Ops:
  34.8 98.0 %all-to-all-start = ((f32[32,256,128]{2,0,1:T(8,128)}), f32[32,256,128]{2,0,1:T(8,128)}, u32[]{:S(2)}, u32[]{:S(2)}) async-start(f32[32,256,128]{2,0,1:T(8,128)} %copy.116), calls=%async_computation | async-start | bytes 8388608 | tf_op jit(solution)/shard_map/all_to_all | solution.py:74
  132.8 97.1 %all-to-all-start.1 = ((f32[32,256,128]{2,0,1:T(8,128)}), f32[32,256,128]{2,0,1:T(8,128)}, u32[]{:S(2)}, u32[]{:S(2)}) async-start(f32[32,256,128]{2,0,1:T(8,128)} %copy.120), calls=%async_computation.1 | async-start | bytes 8388608 | tf_op jit(solution)/shard_map/all_to_all | solution.py:74
  137.4 339.9 %reduce-scatter.6.cloned.1.call-start = ((), (), s32[]{:S(2)}) async-start(), calls=%async_computation.12 | async-start | bytes 5242880 | tf_op jit(solution)/shard_map/reduce_scatter | solution.py:85
  255.6 97.1 %all-to-all-start.3 = ((f32[32,256,128]{2,0,1:T(8,128)}), f32[32,256,128]{2,0,1:T(8,128)}, u32[]{:S(2)}, u32[]{:S(2)}) async-start(f32[32,256,128]{2,0,1:T(8,128)} %copy.132), calls=%async_computation.5 | async-start | bytes 8388608 | tf_op jit(solution)/shard_map/all_to_all | solution.py:74
  352.7 97.1 %all-to-all-start.2 = ((f32[32,256,128]{2,0,1:T(8,128)}), f32[32,256,128]{2,0,1:T(8,128)}, u32[]{:S(2)}, u32[]{:S(2)}) async-start(f32[32,256,128]{2,0,1:T(8,128)} %copy.128), calls=%async_computation.4 | async-start | bytes 8388608 | tf_op jit(solution)/shard_map/all_to_all | solution.py:74
  357.3 121.6 %reduce-scatter.8.cloned.1.call-start = ((), (), s32[]{:S(2)}) async-start(), calls=%async_computation.13 | async-start | bytes 5242880 | tf_op jit(solution)/shard_map/reduce_scatter | solution.py:86
  366.4 141.3 %reduce-scatter.12.cloned.1.call-start = ((), (), s32[]{:S(2)}) async-start(), calls=%async_computation.15 | async-start | bytes 5242880 | tf_op jit(solution)/shard_map/reduce_scatter | solution.py:86
  463.2 91.5 %reduce-scatter.10.cloned.1.call-start = ((), (), s32[]{:S(2)}) async-start(), calls=%async_computation.14 | async-start | bytes 5242880 | tf_op jit(solution)/shard_map/reduce_scatter | solution.py:85
  569.1 53.0 %all-to-all-start.4 = ((f32[256,8,256]{2,1,0:T(8,128)}), f32[256,8,256]{2,1,0:T(8,128)}, u32[]{:S(2)}, u32[]{:S(2)}) async-start(f32[256,8,256]{2,1,0:T(8,128)} %copy.150), calls=%async_computation.8 | async-start | bytes 4194304 | tf_op jit(solution)/shard_map/all_to_all | solution.py:95
  622.1 52.1 %all-to-all-start.5 = ((f32[256,8,256]{2,1,0:T(8,128)}), f32[256,8,256]{2,1,0:T(8,128)S(1)}, u32[]{:S(2)}, u32[]{:S(2)}) async-start(f32[256,8,256]{2,1,0:T(8,128)} %copy.156), calls=%async_computation.9 | async-start | bytes 4194304 | tf_op jit(solution)/shard_map/all_to_all | solution.py:95
  626.7 171.4 %reduce-scatter.14.cloned.1.call-start = ((), (), s32[]{:S(2)}) async-start(), calls=%async_computation.16 | async-start | bytes 10485760 | tf_op jit(solution)/shard_map/reduce_scatter | solution.py:109
  696.1 156.4 %all-to-all-start.6 = ((f32[1,32,256,256]{3,1,0,2:T(8,128)}), f32[1,32,256,256]{3,1,0,2:T(8,128)}, u32[]{:S(2)}, u32[]{:S(2)}) async-start(f32[1,32,256,256]{3,1,0,2:T(8,128)} %copy.158), calls=%async_computation.11 | async-start | bytes 16777216 | tf_op jit(solution)/shard_map/all_to_all | solution.py:117
  800.9 38.3 %collective-permute-start = (f32[32,4,256]{2,1,0:T(4,128)S(1)}, f32[32,4,256]{2,1,0:T(4,128)S(1)}, u32[]{:S(2)}, u32[]{:S(2)}) collective-permute-start(f32[32,4,256]{2,1,0:T(4,128)S(1)} %get-tuple-element.43), channel_id=1, source_target_pairs={{0,8},{8,16},{16,24},{1,9},{9,17},{17,25},{2,10},{10,18},{18,26},{... | collective-permute-start | bytes 393224 | tf_op jit(solution)/shard_map/ppermute | solution.py:19
  803.6 37.4 %collective-permute-start.1 = (f32[32,4,256]{2,1,0:T(4,128)S(1)}, f32[32,4,256]{2,1,0:T(4,128)S(1)}, u32[]{:S(2)}, u32[]{:S(2)}) collective-permute-start(f32[32,4,256]{2,1,0:T(4,128)S(1)} %get-tuple-element.44), channel_id=1, source_target_pairs={{8,0},{16,8},{24,16},{9,1},{17,9},{25,17},{10,2},{18,10},{26,18},{... | collective-permute-start | bytes 393224 | tf_op jit(solution)/shard_map/ppermute | solution.py:20
  841.8 22.4 %collective-permute-start.2 = (f32[4,72,256]{2,1,0:T(8,128)}, f32[4,72,256]{2,1,0:T(8,128)S(1)}, u32[]{:S(2)}, u32[]{:S(2)}) collective-permute-start(f32[4,72,256]{2,1,0:T(8,128)} %get-tuple-element.39), channel_id=1, source_target_pairs={{0,1},{1,2},{2,3},{3,4},{4,5},{5,6},{6,7},{8,9},{9,10},{10,11},{11... | collective-permute-start | bytes 884744 | tf_op jit(solution)/shard_map/ppermute | solution.py:19
  844.2 20.0 %collective-permute-start.3 = (f32[4,72,256]{2,1,0:T(8,128)S(1)}, f32[4,72,256]{2,1,0:T(8,128)}, u32[]{:S(2)}, u32[]{:S(2)}) collective-permute-start(f32[4,72,256]{2,1,0:T(8,128)S(1)} %get-tuple-element.40), channel_id=1, source_target_pairs={{1,0},{2,1},{3,2},{4,3},{5,4},{6,5},{7,6},{9,8},{10,9},{11,10},{12... | collective-permute-start | bytes 884744 | tf_op jit(solution)/shard_map/ppermute | solution.py:20
  912.2 8.5 collective-permute-start.4
  914.5 9.2 collective-permute-start.5
  929.5 6.3 collective-permute-start.7
  939.3 6.3 collective-permute-start.9
  945.6 9.5 collective-permute-start.10
  947.6 14.0 %collective-permute-start.11 = (f32[4,72,256]{2,1,0:T(8,128)S(1)}, f32[4,72,256]{2,1,0:T(8,128)S(1)}, u32[]{:S(2)}, u32[]{:S(2)}) collective-permute-start(f32[4,72,256]{2,1,0:T(8,128)S(1)} %get-tuple-element.36), channel_id=1, source_target_pairs={{1,0},{2,1},{3,2},{4,3},{5,4},{6,5},{7,6},{9,8},{10,9},{11,10},{12... | collective-permute-start | bytes 884744 | tf_op jit(solution)/shard_map/ppermute | solution.py:20
  1014.8 11.0 %collective-permute-start.12 = (f32[4,72,256]{2,1,0:T(8,128)S(1)}, f32[4,72,256]{2,1,0:T(8,128)S(1)}, u32[]{:S(2)}, u32[]{:S(2)}) collective-permute-start(f32[4,72,256]{2,1,0:T(8,128)S(1)} %copy.222), channel_id=1, source_target_pairs={{0,1},{1,2},{2,3},{3,4},{4,5},{5,6},{6,7},{8,9},{9,10},{10,11},{11... | collective-permute-start | bytes 884744 | tf_op jit(solution)/shard_map/ppermute | solution.py:43
  1016.8 16.1 %collective-permute-start.13 = (f32[4,72,256]{2,1,0:T(8,128)S(1)}, f32[4,72,256]{2,1,0:T(8,128)S(1)}, u32[]{:S(2)}, u32[]{:S(2)}) collective-permute-start(f32[4,72,256]{2,1,0:T(8,128)S(1)} %copy.223), channel_id=1, source_target_pairs={{1,0},{2,1},{3,2},{4,3},{5,4},{6,5},{7,6},{9,8},{10,9},{11,10},{12... | collective-permute-start | bytes 884744 | tf_op jit(solution)/shard_map/ppermute | solution.py:44
  (95 other events, 563.0 us)
Sparse Core Ops, SparseCore 0:
  242.6 44.3 reduce-scatter.5
  366.5 46.5 reduce-scatter.7
  463.3 44.3 reduce-scatter.11
  510.1 44.5 reduce-scatter.9
  682.7 115.3 reduce-scatter.13
where the time goes:
time: 1060 us; the launch traced here: 1050 us
  waiting for transfers between devices  580 us (55%)
  matrix products  259 us (24%)
  local copies, waits for them, and re-layouts  95 us (9%)
  starting transfers between devices  80.9 us (8%)
  other arithmetic  20 us (2%)
  between operations  16.2 us (2%)
    all_to_all x4, waiting for transfers between devices, joined_of(): lax.all_to_all(piece, 'pencil', split_axis=1, concat_axis=0, tiled=True)  283 us
    dot_general x38, matrix products, mix(): return jnp.einsum(form, left, right, precision=lax.Precision.HIGH)  240 us
    reduce_scatter x1, waiting for transfers between devices, joined_of(): return lax.psum_scatter(partial, 'view', scatter_dimension=1, tiled=True)  91 us
    all_to_all x2, waiting for transfers between devices, joined_of(): lax.all_to_all(piece, 'pencil', split_axis=0, concat_axis=1, tiled=True)  79 us
    ppermute x4, waiting for transfers between devices, padded_2(): before = lax.ppermute(last, axis, up)  34 us
    unnamed x188, local copies, waits for them, and re-layouts  33.9 us
    reduce_scatter x2, waiting for transfers between devices, joined_of(): real = lax.psum_scatter(out_real, 'view', scatter_dimension=1, tiled=True)  30.1 us
    reduce_scatter x2, waiting for transfers between devices, joined_of(): imag = lax.psum_scatter(out_imag, 'view', scatter_dimension=1, tiled=True)  27.2 us
  transfers between devices with their start and end apart: 28, of which 20 were waited for; matrix products, arithmetic and copies ran while one was open for 19% of the time, Pallas kernels for 0%

commit v1 on v0

v1 whole, which is shorter than its diff:
```python
import functools
import math

import jax
import jax.numpy as jnp
from jax import lax
from jax.experimental import pallas as pl
from jax.experimental.pallas import tpu as pltpu
from jax.sharding import PartitionSpec as P

ITERS = 2
MESH = pl.DeviceIdType.MESH


def mix(form, left, right):
    return jnp.einsum(form, left, right, precision=lax.Precision.HIGH)


def turns(first, second, length):
    product = first[:, None] * second[None, :] % length
    phases = product.astype(jnp.float32) * (2.0 * math.pi / length)
    return (jnp.cos(phases), jnp.sin(phases))


def rotation(cos, sin):
    return jnp.stack([jnp.stack([cos, sin]), jnp.stack([-sin, cos])])


def exchange(parts, axis):
    count = len(parts)
    got = [parts[0]]
    for step in range(1, count):
        pairs = [(i, (i + step) % count) for i in range(count)]
        got.append(lax.ppermute(parts[step], axis, pairs))
    return got


def flat_rows(value, width):
    flat = value.reshape(-1)
    rest = -flat.shape[0] % width
    return jnp.pad(flat, (0, rest)).reshape(-1, width)


def padded_2(shard, sides, width):
    for axis, dim in sides:
        devices, length = (lax.axis_size(axis), shard.shape[dim])
        up = [(i, (i + 1) % devices) for i in range(devices - 1)]
        down = [(j, i) for i, j in up]
        last = lax.slice_in_dim(shard, length - width, length, axis=dim)
        leading = lax.slice_in_dim(shard, 0, width, axis=dim)
        before = lax.ppermute(last, axis, up)
        after = lax.ppermute(leading, axis, down)
        shard = jnp.concatenate([before, shard, after], axis=dim)
    return shard


def folded(full, axis, dim, width):
    devices, length = (lax.axis_size(axis), full.shape[dim] - 2 * width)
    up = [(i, (i + 1) % devices) for i in range(devices - 1)]
    down = [(j, i) for i, j in up]
    before = lax.slice_in_dim(full, 0, width, axis=dim)
    after = lax.slice_in_dim(full, length + width, length + 2 * width, axis=dim)
    own = lax.slice_in_dim(full, width, length + width, axis=dim)
    from_below = lax.ppermute(after, axis, up)
    from_above = lax.ppermute(before, axis, down)
    spread = [(0, 0, 0)] * full.ndim
    spread[dim] = (0, length - width, 0)
    lower = lax.pad(from_below, jnp.float32(0), spread)
    spread[dim] = (length - width, 0, 0)
    return own + lower + lax.pad(from_above, jnp.float32(0), spread)


def band(taps, rows, columns, shift):
    offset = jnp.arange(columns)[None, :] - jnp.arange(rows)[:, None] + shift
    total = jnp.zeros((taps.shape[0], rows, columns), jnp.float32)
    for t in range(taps.shape[1]):
        total = total + jnp.where(offset == t, taps[:, t, None, None], 0.0)
    return total


def parts_of(value):
    high = lax.reduce_precision(value, 8, 7)
    return high.astype(jnp.bfloat16), (value - high).astype(jnp.bfloat16)


def thrice(table_high, table_low, value):
    high = value.astype(jnp.bfloat16)
    low = (value - high.astype(jnp.float32)).astype(jnp.bfloat16)
    total = jnp.dot(table_high, high, preferred_element_type=jnp.float32)
    total += jnp.dot(table_low, high, preferred_element_type=jnp.float32)
    return total + jnp.dot(table_high, low, preferred_element_type=jnp.float32)


def spectral_kernel(
    views, pencils, chunks,
    sent, recorded, weight, turn_high, turn_low, back_high, back_low, picks, out, stacked,
    landed, high, low, product, terms, inverse,
    sent_sem, landed_sem, kept_sem, view_send, view_recv, back_send, back_recv, back_kept,
    share_send, share_recv, share_kept,
):
    view, me = lax.axis_index("view"), lax.axis_index("pencil")
    lines, nz, half = stacked.shape[2], weight.shape[2], weight.shape[3]
    rows = out.shape[2]
    mine = pl.ds(pl.multiple_of(me * rows, rows), rows)
    step = 2 - landed.shape[2] % 2

    barrier = pltpu.get_barrier_semaphore()

    @pl.loop(1, pencils)
    def _(d):
        pl.semaphore_signal(barrier, inc=1, device_id=(view, lax.rem(me + d, pencils)), device_id_type=MESH)

    @pl.loop(1, views)
    def _(d):
        pl.semaphore_signal(barrier, inc=1, device_id=(lax.rem(view + d, views), me), device_id_type=MESH)

    pl.semaphore_wait(barrier, pencils - 1 + views - 1)

    def forward(j, d):
        to = lax.rem(me + d, pencils)
        return pltpu.make_async_remote_copy(
            src_ref=sent.at[:, to, j], dst_ref=landed.at[j, :, :, me],
            send_sem=sent_sem.at[j, d], recv_sem=landed_sem.at[j, d],
            device_id=(view, to), device_id_type=MESH,
        )

    def kept(j):
        return pltpu.make_async_copy(sent.at[:, me, j], landed.at[j, :, :, me], kept_sem.at[j])

    def share(d):
        to = lax.rem(view + d, views)
        theirs = pl.ds(pl.multiple_of(to * lines, lines), lines)
        return pltpu.make_async_remote_copy(
            src_ref=recorded.at[0, :, theirs, :], dst_ref=stacked.at[view],
            send_sem=share_send.at[d], recv_sem=share_recv.at[d],
            device_id=(to, me), device_id_type=MESH,
        )

    def share_own():
        ours = pl.ds(pl.multiple_of(view * lines, lines), lines)
        return pltpu.make_async_copy(recorded.at[0, :, ours, :], stacked.at[view], share_kept)

    def across(j, d):
        to = lax.rem(view + d, views)
        return pltpu.make_async_remote_copy(
            src_ref=product.at[j, to], dst_ref=terms.at[j, d],
            send_sem=view_send.at[j, d], recv_sem=view_recv.at[j, d],
            device_id=(to, me), device_id_type=MESH,
        )

    def backward(j, d):
        to = lax.rem(me + d, pencils)
        theirs = pl.ds(pl.multiple_of(to * rows, rows), rows)
        return pltpu.make_async_remote_copy(
            src_ref=inverse.at[j, theirs, :], dst_ref=out.at[j, me],
            send_sem=back_send.at[j, d], recv_sem=back_recv.at[j, d],
            device_id=(view, to), device_id_type=MESH,
        )

    def back_own(j):
        return pltpu.make_async_copy(inverse.at[j, mine, :], out.at[j, me], back_kept.at[j])

    @pl.loop(0, chunks)
    def _(j):
        @pl.loop(1, pencils)
        def _(d):
            forward(j, d).start()

        kept(j).start()

    @pl.loop(1, views)
    def _(d):
        share(d).start()

    share_own().start()

    def finish(j):
        total = product[j, view]
        for d in range(1, views):
            across(j, d).wait_recv()
            total = total + terms[j, d]
        inverse[j] = thrice(back_high[...], back_low[...], total)

        @pl.loop(1, pencils)
        def _(d):
            backward(j, d).start()

        back_own(j).start()

    @pl.loop(0, chunks)
    def _(j):
        @pl.loop(1, pencils)
        def _(d):
            forward(j, d).wait_recv()

        kept(j).wait()

        for r in range(0, landed.shape[2], step):
            field = jnp.concatenate([
                jnp.concatenate([landed[j, c, r + i].reshape(nz, half) for i in range(step)], axis=1)
                for c in range(2)
            ], axis=0)
            spectrum = thrice(turn_high[...], turn_low[...], field)
            factor = jnp.concatenate([weight[j, r + i] for i in range(step)], axis=1)
            columns = slice(r * half, (r + step) * half)
            for c in range(2):
                part = spectrum[c * nz:(c + 1) * nz] * factor
                coarse = part.astype(jnp.bfloat16)
                high[c * nz:(c + 1) * nz, columns] = coarse
                low[c * nz:(c + 1) * nz, columns] = (part - coarse.astype(jnp.float32)).astype(jnp.bfloat16)

        @pl.loop(1, views + 1)
        def _(d):
            to = lax.rem(view + d, views)
            moved = jnp.dot(high[...], picks[to], preferred_element_type=jnp.float32)
            product[j, to] = moved + jnp.dot(low[...], picks[to], preferred_element_type=jnp.float32)

            @pl.when(d < views)
            def _():
                across(j, d).start()

        @pl.when(j > 0)
        def _():
            finish(j - 1)

    finish(chunks - 1)

    @pl.loop(0, chunks)
    def _(j):
        @pl.loop(1, pencils)
        def _(d):
            forward(j, d).wait_send()
            backward(j, d).wait()

        @pl.loop(1, views)
        def _(d):
            across(j, d).wait_send()

        back_own(j).wait()

    @pl.loop(1, views)
    def _(d):
        share(d).wait()

    share_own().wait()


def spectral(sent, recorded, weight, turn, back):
    views = lax.axis_size("view")
    _, pencils, chunks, block, depth, half = sent.shape
    whole, dma = pl.BlockSpec(memory_space=pltpu.VMEM), pltpu.SemaphoreType.DMA
    anywhere = pl.BlockSpec(memory_space=pl.ANY)
    total, quarter, lines = turn.shape[0], half // views, recorded.shape[2] // views
    lanes = block * quarter
    source, target = jnp.arange(block * half), jnp.arange(lanes)
    target = target // quarter * half + target % quarter
    target = target[None, :] + jnp.arange(views)[:, None] * quarter
    picks = (source[None, :, None] == target[:, None, :]).astype(jnp.bfloat16)
    return pl.pallas_call(
        functools.partial(spectral_kernel, views, pencils, chunks),
        out_shape=(
            jax.ShapeDtypeStruct((chunks, pencils, 2 * depth, lanes), jnp.float32),
            jax.ShapeDtypeStruct((views, depth, lines, recorded.shape[3]), jnp.float32),
        ),
        in_specs=[anywhere] * 2 + [whole] * 6,
        out_specs=(anywhere, anywhere),
        scratch_shapes=[
            pltpu.VMEM((chunks, 2, block, pencils, depth, half), jnp.float32),
            pltpu.VMEM((total, block * half), jnp.bfloat16),
            pltpu.VMEM((total, block * half), jnp.bfloat16),
            pltpu.VMEM((chunks, views, total, lanes), jnp.float32),
            pltpu.VMEM((chunks, views, total, lanes), jnp.float32),
            pltpu.VMEM((chunks, total, lanes), jnp.float32),
            dma((chunks, pencils)), dma((chunks, pencils)), dma((chunks,)),
            dma((chunks, views)), dma((chunks, views)),
            dma((chunks, pencils)), dma((chunks, pencils)), dma((chunks,)),
            dma((views,)), dma((views,)), dma,
        ],
        compiler_params=pltpu.CompilerParams(
            collective_id=0, has_side_effects=True, vmem_limit_bytes=60 << 20,
        ),
        cost_estimate=pl.CostEstimate(flops=10 ** 10, bytes_accessed=1 << 25, transcendentals=0),
    )(sent, recorded, weight, *parts_of(turn), *parts_of(back), picks)


def mirrored_weights(weights, half, chunks):
    pencils = lax.axis_size("pencil")
    nz, block, _ = weights.shape
    rows = block // chunks
    mirror = [(i, pencils - 1 - i) for i in range(pencils)]
    wrapped = [(i, (pencils - i) % pencils) for i in range(pencils)]
    positions, lanes = jnp.arange(nz), jnp.arange(half)
    flip_z = (positions[:, None] == (nz - positions[None, :]) % nz).astype(jnp.float32)
    flip_x = 0.5 * (lanes[:, None] == half - lanes[None, :]).astype(jnp.float32)
    share = jnp.where(lanes == 0, 1.0, 0.5)
    result = []
    for j in range(chunks):
        high = block - j * rows + 1
        if j == 0:
            upper = jnp.concatenate([weights[:, high - rows:high - 1, half:], weights[:, :1, half:]], axis=1)
        else:
            upper = weights[:, high - rows:high, half:]
        facing = mix("zrl,lx->rzx", jnp.flip(upper, axis=1), flip_x)
        facing = mix("zk,rzx->rkx", flip_z, facing)
        if j == 0:
            edge = lax.ppermute(facing[0], "pencil", wrapped)
        facing = lax.ppermute(facing, "pencil", mirror)
        if j == 0:
            facing = jnp.concatenate([edge[None], facing[1:]], axis=0)
        own = weights[:, j * rows:(j + 1) * rows, :half] * share
        result.append(own.transpose(1, 0, 2) + facing)
    return jnp.stack(result)


def nyquist_of(slab, weights, half, table_to, turn_z, back_z, table_from):
    signs = 1.0 - 2.0 * (jnp.arange(slab.shape[2]) % 2).astype(jnp.float32)
    depth, ny = slab.shape[:2]
    pencils = lax.axis_size("pencil")
    line = mix("dky,zy->zdk", table_to, jnp.sum(slab * signs, axis=-1))
    line = line.reshape(depth * 2, pencils, ny // pencils).swapaxes(0, 1)
    line = lax.all_to_all(line, "pencil", split_axis=0, concat_axis=0, tiled=True)
    line = line.reshape(pencils * depth, 2, ny // pencils)
    line = mix("dckz,zcy->dky", turn_z, line) * weights[:, :, half]
    line = mix("dczk,cky->zdy", back_z, line)
    line = line.reshape(pencils, depth * 2, ny // pencils)
    line = lax.all_to_all(line, "pencil", split_axis=0, concat_axis=0, tiled=True)
    line = line.reshape(pencils, depth, 2, ny // pencils)
    return mix("pzcb,cypb->zy", line, table_from)


def joined_of(recorded, weights):
    slab = recorded[0]
    views, pencils = lax.axis_size("view"), lax.axis_size("pencil")
    view = lax.axis_index("view")
    depth, ny, nx = slab.shape
    nz, block = weights.shape[:2]
    half, lines = nx // 2, ny // views
    quarter = half // views
    chunks = max(1, block * quarter // 256)
    rows = block // chunks
    halves = mirrored_weights(weights, half, chunks)

    to_view = lax.rem(view + jnp.arange(views, dtype=jnp.int32), views)
    source_view = lax.rem(view - jnp.arange(views, dtype=jnp.int32) + views, views)

    def spots(blocks, size):
        return (blocks[:, None] * size + jnp.arange(size, dtype=jnp.int32)[None, :]).reshape(-1)

    all_x, all_y = jnp.arange(nx, dtype=jnp.int32), jnp.arange(ny, dtype=jnp.int32)
    all_z = jnp.arange(nz, dtype=jnp.int32)
    cos_x, sin_x = turns(jnp.arange(half, dtype=jnp.int32), all_x, nx)
    rolled = mix("zyx,ckx->zcyk", slab, jnp.stack([cos_x, -sin_x]))
    cos_y, sin_y = turns(all_y, all_y, ny)
    piece = mix("dcky,zcyx->dkzx", rotation(cos_y, sin_y), rolled)
    piece = piece.reshape(2, pencils, chunks, rows, depth, half)

    cos_z, sin_z = turns(all_z, all_z, nz)
    turn_z, back_z = rotation(cos_z, sin_z), rotation(cos_z, -sin_z)
    turn = turn_z.transpose(0, 2, 1, 3).reshape(2 * nz, 2 * nz)
    back = back_z.reshape(2, 2, pencils, depth, nz).transpose(2, 0, 3, 1, 4).reshape(2 * nz, 2 * nz)
    cos_v, sin_v = turns(spots(to_view, lines), all_y, ny)
    back_y = rotation(cos_v, -sin_v).reshape(2, 2, views, lines, pencils, chunks, rows)
    edge = nyquist_of(
        slab, weights, half, jnp.stack([cos_y, -sin_y]), turn_z, back_z,
        jnp.stack([cos_v, -sin_v]).reshape(2, ny, pencils, block),
    ).reshape(depth, views, lines)
    got, stacked = spectral(piece, recorded, halves, turn, back)
    got = got.reshape(chunks, pencils, 2, depth, rows, quarter)
    spread = mix("jpczrx,dcvypjr->vzxdy", got, back_y)
    spread = spread.reshape(views, depth * quarter, 2 * lines)
    parts = [
        jnp.concatenate([spread[d], flat_rows(edge[:, d], 2 * lines)], axis=0)
        for d in range(views)
    ]
    parts = exchange(parts, "view")
    main = depth * quarter
    line = sum(part[main:].reshape(-1)[:depth * lines] for part in parts).reshape(depth, lines)
    spread = jnp.stack([part[:main].reshape(depth, quarter, 2, lines) for part in parts])
    scale = 1.0 / float(nz * ny * nx)
    waves = spots(source_view, quarter)
    cos_x, sin_x = turns(waves, all_x, nx)
    weight = jnp.where(waves == 0, scale, 2.0 * scale)[:, None]
    table = jnp.stack([cos_x * weight, -sin_x * weight]).reshape(2, views, quarter, nx)
    signs = 1.0 - 2.0 * (all_x % 2).astype(jnp.float32)
    joined = mix("vzkcy,cvkx->zyx", spread, table) + line[:, :, None] * (signs * scale)
    return joined, stacked


def body(recorded, spectral_weight, psf_taps):
    view_count = lax.axis_size("view")
    joined_volume, stacked = joined_of(recorded, spectral_weight[0])
    kernels = psf_taps / jnp.sum(psf_taps, axis=-1, keepdims=True)
    margin = kernels.shape[-1] // 2
    depth, rows, length = joined_volume.shape
    blur_z = band(kernels[:, 0], depth, depth + 2 * margin, 0)
    blur_y = band(kernels[:, 1], rows, rows + 2 * margin, 0)
    blur_x = band(kernels[:, 2], length, length, margin)
    local = 0.1 + jax.nn.softplus(joined_volume)
    for repeat in range(ITERS):
        padded = padded_2(local, (("view", 1), ("pencil", 0)), margin)
        field = mix("vza,abx->vzbx", blur_z, padded)
        field = mix("vyb,vzbx->vzyx", blur_y, field)
        ratio = stacked / mix("vzyx,vcx->vzyc", field, blur_x)
        field = mix("vzyc,vcx->vzyx", ratio, blur_x)
        field = mix("vyb,vzyx->vzbx", blur_y, field)
        total = mix("vza,vzbx->abx", blur_z, field)
        total = folded(folded(total, "pencil", 0, margin), "view", 1, margin)
        local = local * total / view_count
    return (joined_volume, local)


def solution(mesh):
    return jax.shard_map(
        body,
        mesh=mesh,
        in_specs=(P("view", "pencil", None, None), P("view", None, "pencil", None), P()),
        out_specs=(P("pencil", "view", None), P("pencil", "view", None)),
        check_vma=False,
    )
```

time: 1060 us -> 746 us (0.70)
  waiting for transfers between devices: 580 us -> 151 us
  Pallas kernels: 0 us -> 236 us
  matrix products: 259 us -> 147 us
  local copies, waits for them, and re-layouts: 95 us -> 58.2 us
  other arithmetic: 20 us -> 48.4 us
  between operations: 16.2 us -> 2.74 us
    all_to_all x7 -> x2, waiting for transfers between devices: 362 us -> 96.9 us  [nyquist_of(): lax.all_to_all(line, 'pencil', split_axis=0, concat_axis=0, tiled=True)]
    pallas_call x0 -> x1, Pallas kernels: none -> 236 us  [spectral(): pl.pallas_call(functools.partial(spectral_kernel, views, pencils, chunks)...]
    reduce_scatter x5 -> x0, waiting for transfers between devices: 148 us -> none  [the longest x1 91 us: joined_of(): return lax.psum_scatter(partial, 'view', scatter_dimension=1, tiled=True)]
    dot_general x38 -> x28, matrix products: 240 us -> 147 us  [mix(): return jnp.einsum(form, left, right, precision=lax.Precision.HIGH)]
    all_to_all x7 -> x2, starting transfers between devices: 35.7 us -> 12.1 us  [nyquist_of(): lax.all_to_all(line, 'pencil', split_axis=0, concat_axis=0, tiled=True)]
    all_to_all x5 -> x3, local copies, waits for them, and re-layouts: 24.8 us -> 1.69 us  [nyquist_of(): lax.all_to_all(line, 'pencil', split_axis=0, concat_axis=0, tiled=True)]
    unnamed x188 -> x161, local copies, waits for them, and re-layouts: 33.9 us -> 12 us
    ppermute x4, waiting for transfers between devices: 34 us -> 12.3 us  [padded_2(): before = lax.ppermute(last, axis, up)]
  transfers between devices with their start and end apart: 28 -> 26, of which waited for: 20 -> 19; matrix products, arithmetic and copies ran while one was open for 19% -> 13% of each run, Pallas kernels for 0% -> 0%
where the time goes in v1:
time: 746 us; the launch traced here: 733 us
  Pallas kernels  236 us (32%)
  waiting for transfers between devices  151 us (20%)
  matrix products  147 us (20%)
  starting transfers between devices  89.8 us (12%)
  local copies, waits for them, and re-layouts  58.2 us (8%)
  other arithmetic  48.4 us (6%)
    pallas_call x1, Pallas kernels, spectral(): pl.pallas_call(functools.partial(spectral_kernel, views, pencils, chunks)...  236 us
    dot_general x28, matrix products, mix(): return jnp.einsum(form, left, right, precision=lax.Precision.HIGH)  147 us
    all_to_all x2, waiting for transfers between devices, nyquist_of(): lax.all_to_all(line, 'pencil', split_axis=0, concat_axis=0, tiled=True)  96.9 us
    ppermute x4, starting transfers between devices, folded(): from_above = lax.ppermute(before, axis, down)  19.3 us
    ppermute x4, starting transfers between devices, padded_2(): after = lax.ppermute(leading, axis, down)  16.6 us
    ppermute x3, waiting for transfers between devices, exchange(): got.append(lax.ppermute(parts[step], axis, pairs))  16.1 us
  transfers between devices with their start and end apart: 26, of which 19 were waited for; matrix products, arithmetic and copies ran while one was open for 13% of the time, Pallas kernels for 0%

profile of v1, /device:TPU:25, one launch (start us, length us, event | category | flops | bytes accessed | tf_op | source)
XLA Modules:
  0.0 733.0 jit_solution(10454648280739507021)
XLA Ops:
  14.2 8.2 %copy.192 = f32[1,256,32,256]{3,1,2,0:T(8,128)S(1)} copy(f32[1,256,32,256]{3,2,1,0:T(8,128)} %param.4) | data formatting | bytes 16777216 | tf_op args[1]
  60.1 6.3 fusion.10
  66.6 9.8 %fusion.32 = f32[2,256,32,128]{3,1,2,0:T(8,128)} fusion(f32[2,128,32,256]{3,1,0,2:T(8,128)S(1)} %fusion.10, f32[1,2,256,256]{3,2,1,0:T(8,128)S(1)} %get-tuple-element.62, f32[1,2,256,256]{3,2,1,0:T(8,128)S(1)} %get-tuple-element.65), kind=kOutput, calls=%fused_computation.40 | convolution fusion | flops 6442713088 | bytes 17825792 | tf_op jit(solution)/shard_map/dcky,zcyx->dkzx/dot_general | solution.py:16
  90.0 11.5 %copy.86 = f32[2,256,32,128]{3,2,1,0:T(8,128)} copy(f32[2,256,32,128]{3,1,2,0:T(8,128)} %fusion.32) | data formatting | bytes 16777216 | tf_op jit(solution)/shard_map/dcky,zcyx->dkzx/dot_general | solution.py:16
  109.7 6.6 all-to-all-start.1
  116.3 96.9 %all-to-all-done.1 = f32[8,1,2048]{2,1,0:T(1,128)S(1)} async-done(((f32[8,1,2048]{2,1,0:T(1,128)}), f32[8,1,2048]{2,1,0:T(1,128)S(1)}, u32[]{:S(2)}, u32[]{:S(2)}) %all-to-all-start.1) | async-done | bytes 65568 | tf_op jit(solution)/shard_map/all_to_all | solution.py:326
  223.2 235.8 %shard_map.50 = (f32[4,8,64,256]{3,2,1,0:T(8,128)}, f32[4,32,64,256]{3,2,1,0:T(8,128)}) custom-call(f32[2,8,4,8,32,128]{5,4,3,2,1,0:T(8,128)} %bitcast.273, f32[1,32,256,256]{3,2,1,0:T(8,128)} %recorded.1, f32[4,8,256,128]{3,2,1,0:T(8,128)} %pad_maximum_fusion.weight, bf16[512,512]{1,0:T(8,128)(2,1)} %get-tuple-element.60.turn_high, ...), custom_call_target="tpu_custom_call" | custom-call | flops 10000000000 | bytes 33554432 | tf_op jit(solution)/shard_map/pallas_call | solution.py:259
  459.0 6.0 reshape.787
  465.0 10.6 %fusion.43 = f32[4,32,32,2,64]{4,2,1,0,3:T(8,128)S(1)} fusion(f32[1,1,4,64,8,4,8]{3,6,4,5,1,2,0:T(8,128)S(1)} %copy-done.2, f32[1,1,4,64,8,4,8]{3,6,4,5,1,2,0:T(8,128)S(1)} %get-tuple-element.71, f32[1,1,4,64,8,4,8]{3,6,4,5,1,2,0:T(8,128)S(1)} %get-tuple-element.70, f32[4,8,2,32,8,32]{5,4,3,2,1,0:T(8,128)} %reshape.787), kind=kOutput, calls=%fused_computation.53 | convolution fusion | flops 1611399168 | bytes 4980736 | tf_op jit(solution)/shard_map/jpczrx,dcvypjr->vzxdy/dot_general | solution.py:16
  494.5 6.5 collective-permute-done.6
  501.0 9.6 %collective-permute-done.5 = f32[1040,128]{1,0:T(8,128)S(1)} collective-permute-done((f32[1040,128]{1,0:T(8,128)}, f32[1040,128]{1,0:T(8,128)S(1)}, u32[]{:S(2)}, u32[]{:S(2)}) %collective-permute-start.5) | collective-permute-done | bytes 532512 | tf_op jit(solution)/shard_map/ppermute | solution.py:34
  518.0 7.6 %fusion.46 = (f32[32,64,256]{2,1,0:T(8,128)S(1)}, f32[32,64,256]{2,1,0:T(8,128)}) fusion(f32[256]{0:T(256)S(1)} %broadcast_multiply_fusion, f32[32,64]{1,0:T(8,128)S(1)} %fusion.210, f32[1,4,32,256]{3,2,1,0:T(8,128)S(1)} %get-tuple-element.79, f32[1,4,32,256]{3,2,1,0:T(8,128)S(1)} %get-tuple-element.78, f32[1,32,32,2,64]{4,2,1,0,3:T(8,128)S(1)} %copy.110, ...), kind=kOutput, calls=%fused_computation.54 | convolution fusion | flops 811663360 | bytes 6562816 | tf_op jit(solution)/shard_map/vzkcy,cvkx->zyx/dot_general | solution.py:16
  533.8 6.5 collective-permute-start.11
  554.8 9.7 %fusion.6 = f32[4,32,256,64]{2,3,1,0:T(8,128)S(1)} fusion(f32[4,32,72,256]{3,1,2,0:T(8,128)S(1)} %fusion.37, f32[4]{0:T(128)S(1)} %copy-done.46, f32[4]{0:T(128)S(1)} %copy-done.44, f32[4]{0:T(128)S(1)} %copy-done.42, f32[4]{0:T(128)S(1)} %copy-done.40, f32[4]{0:T(128)S(1)} %copy-done.38, f32[4]{0:T(128)S(1)} %copy-done.36, f32[4]{0:T(128)S(1)} %copy-done.34, ...), kind=kOutput, calls=%fused_computation.6 | convolution fusion | flops 906283008 | bytes 17867408 | tf_op jit(solution)/shard_map/vyb,vzbx->vzyx/dot_general | solution.py:16
  564.6 6.9 fusion.14
  571.4 13.6 %fusion.21 = f32[4,32,64,256]{3,2,1,0:T(8,128)} fusion(f32[4,32,64,256]{3,2,1,0:T(8,128)} %get-tuple-element.5, f32[4,32,64,256]{3,2,1,0:T(8,128)} %fusion.14, f32[4]{0:T(128)S(1)} %copy-done.53, f32[4]{0:T(128)S(1)} %copy-done.55, f32[4]{0:T(128)S(1)} %copy-done.57, f32[4]{0:T(128)S(1)} %copy-done.59, f32[4]{0:T(128)S(1)} %copy-done.61, ...), kind=kOutput, calls=%fused_computation.23 | convolution fusion | flops 3227779072 | bytes 25755792 | tf_op jit(solution)/shard_map/vzyc,vcx->vzyx/dot_general | solution.py:16
  585.0 7.0 convolution_bitcast_fusion.1
  597.9 6.2 collective-permute-start.13
  635.0 6.2 collective-permute-start.19
  655.3 10.6 %fusion.2 = f32[4,32,256,64]{2,3,1,0:T(8,128)} fusion(f32[4,32,72,256]{3,1,2,0:T(8,128)S(1)} %fusion.35, f32[4]{0:T(128)S(1)} %copy-done.47, f32[4]{0:T(128)S(1)} %copy-done.45, f32[4]{0:T(128)S(1)} %copy-done.43, f32[4]{0:T(128)S(1)} %copy-done.41, f32[4]{0:T(128)S(1)} %copy-done.39, f32[4]{0:T(128)S(1)} %copy-done.37, f32[4]{0:T(128)S(1)} %copy-done.35, ...), kind=kOutput, calls=%fused_computation.2 | convolution fusion | flops 906283008 | bytes 17867408 | tf_op jit(solution)/shard_map/vyb,vzbx->vzyx/dot_general | solution.py:16
  666.0 11.1 %fusion.12 = f32[4,32,64,256]{3,2,1,0:T(8,128)} fusion(f32[4,32,256,64]{2,3,1,0:T(8,128)} %fusion.2, f32[4]{0:T(128)S(1)} %copy-done.54, f32[4]{0:T(128)S(1)} %copy-done.56, f32[4]{0:T(128)S(1)} %copy-done.58, f32[4]{0:T(128)S(1)} %copy-done.60, f32[4]{0:T(128)S(1)} %copy-done.62, f32[4]{0:T(128)S(1)} %copy-done.64, f32[4]{0:T(128)S(1)} %copy-done.66, ...), kind=kOutput, calls=%fused_computation.12 | convolution fusion | flops 3225681920 | bytes 17367184 | tf_op jit(solution)/shard_map/vzyx,vcx->vzyc/dot_general | solution.py:16
  677.1 13.6 %fusion.19 = f32[4,32,64,256]{3,2,1,0:T(8,128)} fusion(f32[4,32,64,256]{3,2,1,0:T(8,128)} %get-tuple-element.5, f32[4,32,64,256]{3,2,1,0:T(8,128)} %fusion.12, f32[4]{0:T(128)S(1)} %copy-done.54, f32[4]{0:T(128)S(1)} %copy-done.56, f32[4]{0:T(128)S(1)} %copy-done.58, f32[4]{0:T(128)S(1)} %copy-done.60, f32[4]{0:T(128)S(1)} %copy-done.62, ...), kind=kOutput, calls=%fused_computation.21 | convolution fusion | flops 3227779072 | bytes 25755792 | tf_op jit(solution)/shard_map/vzyc,vcx->vzyx/dot_general | solution.py:16
  690.7 7.0 convolution_bitcast_fusion
  703.8 6.2 collective-permute-start.21
  (338 shorter events, 210.3 us)
Async XLA Ops:
  8.7 92.9 %all-to-all-start = ((f32[8,1,2048]{2,1,0:T(1,128)}), f32[8,1,2048]{2,1,0:T(1,128)}, u32[]{:S(2)}, u32[]{:S(2)}) async-start(f32[8,1,2048]{2,1,0:T(1,128)} %reshape.852), calls=%async_computation | async-start | bytes 131072 | tf_op jit(solution)/shard_map/all_to_all | solution.py:321
  25.1 190.4 %collective-permute-start.1 = (f32[8,256,128]{2,1,0:T(8,128)}, f32[8,256,128]{2,1,0:T(8,128)}, u32[]{:S(2)}, u32[]{:S(2)}) collective-permute-start(f32[8,256,128]{2,1,0:T(8,128)} %convolution_bitcast_fusion.9), channel_id=1, source_target_pairs={{0,7},{1,6},{2,5},{3,4},{4,3},{5,2},{6,1},{7,0},{8,15},{9,14},{10,... | collective-permute-start | bytes 3145736 | tf_op jit(solution)/shard_map/ppermute | solution.py:307
  27.9 188.8 %collective-permute-start = (f32[256,128]{1,0:T(8,128)}, f32[256,128]{1,0:T(8,128)}, u32[]{:S(2)}, u32[]{:S(2)}) collective-permute-start(f32[256,128]{1,0:T(8,128)} %slice_bitcast_fusion), channel_id=1, source_target_pairs={{0,0},{1,7},{2,6},{3,5},{4,4},{5,3},{6,2},{7,1},{8,8},{9,15},{10,1... | collective-permute-start | bytes 393224 | tf_op jit(solution)/shard_map/ppermute | solution.py:306
  33.3 183.4 %collective-permute-start.4 = (f32[8,256,128]{2,1,0:T(8,128)}, f32[8,256,128]{2,1,0:T(8,128)}, u32[]{:S(2)}, u32[]{:S(2)}) collective-permute-start(f32[8,256,128]{2,1,0:T(8,128)} %convolution_bitcast_fusion.6), channel_id=1, source_target_pairs={{0,7},{1,6},{2,5},{3,4},{4,3},{5,2},{6,1},{7,0},{8,15},{9,14},{10,... | collective-permute-start | bytes 3145736 | tf_op jit(solution)/shard_map/ppermute | solution.py:307
  37.3 179.4 %collective-permute-start.3 = (f32[8,256,128]{2,1,0:T(8,128)}, f32[8,256,128]{2,1,0:T(8,128)}, u32[]{:S(2)}, u32[]{:S(2)}) collective-permute-start(f32[8,256,128]{2,1,0:T(8,128)} %convolution_bitcast_fusion.7), channel_id=1, source_target_pairs={{0,7},{1,6},{2,5},{3,4},{4,3},{5,2},{6,1},{7,0},{8,15},{9,14},{10,... | collective-permute-start | bytes 3145736 | tf_op jit(solution)/shard_map/ppermute | solution.py:307
  41.7 175.0 %collective-permute-start.2 = (f32[8,256,128]{2,1,0:T(8,128)}, f32[8,256,128]{2,1,0:T(8,128)}, u32[]{:S(2)}, u32[]{:S(2)}) collective-permute-start(f32[8,256,128]{2,1,0:T(8,128)} %convolution_bitcast_fusion.8), channel_id=1, source_target_pairs={{0,7},{1,6},{2,5},{3,4},{4,3},{5,2},{6,1},{7,0},{8,15},{9,14},{10,... | collective-permute-start | bytes 3145736 | tf_op jit(solution)/shard_map/ppermute | solution.py:307
  109.7 103.5 %all-to-all-start.1 = ((f32[8,1,2048]{2,1,0:T(1,128)}), f32[8,1,2048]{2,1,0:T(1,128)S(1)}, u32[]{:S(2)}, u32[]{:S(2)}) async-start(f32[8,1,2048]{2,1,0:T(1,128)} %reshape.854), calls=%async_computation.1 | async-start | bytes 131072 | tf_op jit(solution)/shard_map/all_to_all | solution.py:326
  481.2 12.5 %collective-permute-start.7 = (f32[1040,128]{1,0:T(8,128)}, f32[1040,128]{1,0:T(8,128)}, u32[]{:S(2)}, u32[]{:S(2)}) collective-permute-start(f32[1040,128]{1,0:T(8,128)} %pad_maximum_fusion.12), channel_id=1, source_target_pairs={{0,24},{8,0},{16,8},{24,16},{1,25},{9,1},{17,9},{25,17},{2,26},{10... | collective-permute-start | bytes 1597448 | tf_op jit(solution)/shard_map/ppermute | solution.py:34
  484.3 16.7 %collective-permute-start.6 = (f32[1040,128]{1,0:T(8,128)}, f32[1040,128]{1,0:T(8,128)S(1)}, u32[]{:S(2)}, u32[]{:S(2)}) collective-permute-start(f32[1040,128]{1,0:T(8,128)} %pad_maximum_fusion.11), channel_id=1, source_target_pairs={{0,16},{8,24},{16,0},{24,8},{1,17},{9,25},{17,1},{25,9},{2,18},{10... | collective-permute-start | bytes 1597448 | tf_op jit(solution)/shard_map/ppermute | solution.py:34
  491.0 19.6 %collective-permute-start.5 = (f32[1040,128]{1,0:T(8,128)}, f32[1040,128]{1,0:T(8,128)S(1)}, u32[]{:S(2)}, u32[]{:S(2)}) collective-permute-start(f32[1040,128]{1,0:T(8,128)} %pad_maximum_fusion.10), channel_id=1, source_target_pairs={{0,8},{8,16},{16,24},{24,0},{1,9},{9,17},{17,25},{25,1},{2,10},{10... | collective-permute-start | bytes 1597448 | tf_op jit(solution)/shard_map/ppermute | solution.py:34
  525.6 6.9 collective-permute-start.9
  527.5 6.2 collective-permute-start.8
  533.8 11.0 %collective-permute-start.11 = (f32[4,72,256]{2,1,0:T(8,128)S(1)}, f32[4,72,256]{2,1,0:T(8,128)S(1)}, u32[]{:S(2)}, u32[]{:S(2)}) collective-permute-start(f32[4,72,256]{2,1,0:T(8,128)S(1)} %get-tuple-element.52), channel_id=1, source_target_pairs={{1,0},{2,1},{3,2},{4,3},{5,4},{6,5},{7,6},{9,8},{10,9},{11,10},{12... | collective-permute-start | bytes 884744 | tf_op jit(solution)/shard_map/ppermute | solution.py:52
  540.4 9.4 %collective-permute-start.10 = (f32[4,72,256]{2,1,0:T(8,128)S(1)}, f32[4,72,256]{2,1,0:T(8,128)S(1)}, u32[]{:S(2)}, u32[]{:S(2)}) collective-permute-start(f32[4,72,256]{2,1,0:T(8,128)S(1)} %get-tuple-element.51), channel_id=1, source_target_pairs={{0,1},{1,2},{2,3},{3,4},{4,5},{5,6},{6,7},{8,9},{9,10},{10,11},{11... | collective-permute-start | bytes 884744 | tf_op jit(solution)/shard_map/ppermute | solution.py:51
  597.9 12.2 %collective-permute-start.13 = (f32[4,72,256]{2,1,0:T(8,128)S(1)}, f32[4,72,256]{2,1,0:T(8,128)S(1)}, u32[]{:S(2)}, u32[]{:S(2)}) collective-permute-start(f32[4,72,256]{2,1,0:T(8,128)S(1)} %copy.149), channel_id=1, source_target_pairs={{1,0},{2,1},{3,2},{4,3},{5,4},{6,5},{7,6},{9,8},{10,9},{11,10},{12... | collective-permute-start | bytes 884744 | tf_op jit(solution)/shard_map/ppermute | solution.py:65
  604.3 10.7 %collective-permute-start.12 = (f32[4,72,256]{2,1,0:T(8,128)S(1)}, f32[4,72,256]{2,1,0:T(8,128)S(1)}, u32[]{:S(2)}, u32[]{:S(2)}) collective-permute-start(f32[4,72,256]{2,1,0:T(8,128)S(1)} %copy.148), channel_id=1, source_target_pairs={{0,1},{1,2},{2,3},{3,4},{4,5},{5,6},{6,7},{8,9},{9,10},{10,11},{11... | collective-permute-start | bytes 884744 | tf_op jit(solution)/shard_map/ppermute | solution.py:64
  616.4 7.6 %collective-permute-start.15 = (f32[32,4,256]{2,1,0:T(4,128)S(1)}, f32[32,4,256]{2,1,0:T(4,128)S(1)}, u32[]{:S(2)}, u32[]{:S(2)}) collective-permute-start(f32[32,4,256]{2,1,0:T(4,128)S(1)} %get-tuple-element.50), channel_id=1, source_target_pairs={{8,0},{16,8},{24,16},{9,1},{17,9},{25,17},{10,2},{18,10},{26,18},{... | collective-permute-start | bytes 393224 | tf_op jit(solution)/shard_map/ppermute | solution.py:65
  626.7 7.0 collective-permute-start.17
  628.7 6.3 collective-permute-start.16
  635.0 10.7 %collective-permute-start.19 = (f32[4,72,256]{2,1,0:T(8,128)S(1)}, f32[4,72,256]{2,1,0:T(8,128)S(1)}, u32[]{:S(2)}, u32[]{:S(2)}) collective-permute-start(f32[4,72,256]{2,1,0:T(8,128)S(1)} %get-tuple-element.48), channel_id=1, source_target_pairs={{1,0},{2,1},{3,2},{4,3},{5,4},{6,5},{7,6},{9,8},{10,9},{11,10},{12... | collective-permute-start | bytes 884744 | tf_op jit(solution)/shard_map/ppermute | solution.py:52
  641.3 9.4 %collective-permute-start.18 = (f32[4,72,256]{2,1,0:T(8,128)S(1)}, f32[4,72,256]{2,1,0:T(8,128)S(1)}, u32[]{:S(2)}, u32[]{:S(2)}) collective-permute-start(f32[4,72,256]{2,1,0:T(8,128)S(1)} %get-tuple-element.47), channel_id=1, source_target_pairs={{0,1},{1,2},{2,3},{3,4},{4,5},{5,6},{6,7},{8,9},{9,10},{10,11},{11... | collective-permute-start | bytes 884744 | tf_op jit(solution)/shard_map/ppermute | solution.py:51
  703.8 12.2 %collective-permute-start.21 = (f32[4,72,256]{2,1,0:T(8,128)S(1)}, f32[4,72,256]{2,1,0:T(8,128)S(1)}, u32[]{:S(2)}, u32[]{:S(2)}) collective-permute-start(f32[4,72,256]{2,1,0:T(8,128)S(1)} %copy.152), channel_id=1, source_target_pairs={{1,0},{2,1},{3,2},{4,3},{5,4},{6,5},{7,6},{9,8},{10,9},{11,10},{12... | collective-permute-start | bytes 884744 | tf_op jit(solution)/shard_map/ppermute | solution.py:65
  710.1 10.7 %collective-permute-start.20 = (f32[4,72,256]{2,1,0:T(8,128)S(1)}, f32[4,72,256]{2,1,0:T(8,128)S(1)}, u32[]{:S(2)}, u32[]{:S(2)}) collective-permute-start(f32[4,72,256]{2,1,0:T(8,128)S(1)} %copy.151), channel_id=1, source_target_pairs={{0,1},{1,2},{2,3},{3,4},{4,5},{5,6},{6,7},{8,9},{9,10},{10,11},{11... | collective-permute-start | bytes 884744 | tf_op jit(solution)/shard_map/ppermute | solution.py:64
  722.2 7.7 %collective-permute-start.23 = (f32[32,4,256]{2,1,0:T(4,128)S(1)}, f32[32,4,256]{2,1,0:T(4,128)S(1)}, u32[]{:S(2)}, u32[]{:S(2)}) collective-permute-start(f32[32,4,256]{2,1,0:T(4,128)S(1)} %get-tuple-element.46), channel_id=1, source_target_pairs={{8,0},{16,8},{24,16},{9,1},{17,9},{25,17},{10,2},{18,10},{26,18},{... | collective-permute-start | bytes 393224 | tf_op jit(solution)/shard_map/ppermute | solution.py:65
  (77 other events, 635.1 us)

commit v2 on v1

--- a/solution.py
+++ b/solution.py
@@ -41,33 +41,229 @@
     return jnp.pad(flat, (0, rest)).reshape(-1, width)
 
 
-def padded_2(shard, sides, width):
-    for axis, dim in sides:
-        devices, length = (lax.axis_size(axis), shard.shape[dim])
-        up = [(i, (i + 1) % devices) for i in range(devices - 1)]
-        down = [(j, i) for i, j in up]
-        last = lax.slice_in_dim(shard, length - width, length, axis=dim)
-        leading = lax.slice_in_dim(shard, 0, width, axis=dim)
-        before = lax.ppermute(last, axis, up)
-        after = lax.ppermute(leading, axis, down)
-        shard = jnp.concatenate([before, shard, after], axis=dim)
-    return shard
-
-
-def folded(full, axis, dim, width):
-    devices, length = (lax.axis_size(axis), full.shape[dim] - 2 * width)
-    up = [(i, (i + 1) % devices) for i in range(devices - 1)]
-    down = [(j, i) for i, j in up]
-    before = lax.slice_in_dim(full, 0, width, axis=dim)
-    after = lax.slice_in_dim(full, length + width, length + 2 * width, axis=dim)
-    own = lax.slice_in_dim(full, width, length + width, axis=dim)
-    from_below = lax.ppermute(after, axis, up)
-    from_above = lax.ppermute(before, axis, down)
-    spread = [(0, 0, 0)] * full.ndim
-    spread[dim] = (0, length - width, 0)
-    lower = lax.pad(from_below, jnp.float32(0), spread)
-    spread[dim] = (length - width, 0, 0)
-    return own + lower + lax.pad(from_above, jnp.float32(0), spread)
+def thrice_right(value, table_high, table_low):
+    high = value.astype(jnp.bfloat16)
+    low = (value - high.astype(jnp.float32)).astype(jnp.bfloat16)
+    total = jnp.dot(high, table_high, preferred_element_type=jnp.float32)
+    total += jnp.dot(high, table_low, preferred_element_type=jnp.float32)
+    return total + jnp.dot(low, table_high, preferred_element_type=jnp.float32)
+
+
+def ratio_kernel(
+    taps, field, recorded, in_high, in_low, right_high, right_low, left_high, left_low, out_high, out_low,
+    total, back,
+):
+    depth, lines, length = recorded.shape
+    view, base = pl.program_id(0), pl.program_id(1) * depth
+    count = taps.shape[1]
+    weights = [taps[view, t] for t in range(count)]
+
+    @pl.when((view == 0) & (base == 0))
+    def _():
+        @pl.loop(0, total.shape[0])
+        def _(z):
+            total[z] = jnp.zeros(total.shape[1:], jnp.float32)
+
+    slices = []
+    for z in range(depth):
+        value = weights[0] * field[base + z]
+        for t in range(1, count):
+            value = value + weights[t] * field[base + z + t]
+        slices.append(thrice(in_high[...], in_low[...], value))
+    blurred = jnp.concatenate(slices, axis=0)
+    blurred = thrice_right(blurred, right_high[...], right_low[...])
+    ratio = recorded[...].reshape(depth * lines, length) / blurred
+    ratio = thrice_right(ratio, left_high[...], left_low[...])
+    for z in range(depth):
+        back[z] = thrice(out_high[...], out_low[...], ratio[z * lines:(z + 1) * lines])
+    for z in range(depth + count - 1):
+        value = total[base + z]
+        for t in range(max(0, z - depth + 1), min(count, z + 1)):
+            value = value + weights[t] * back[z - t]
+        total[base + z] = value
+
+
+def corrections(padded, stacked, taps_z, blur_y, blur_x):
+    views, depth, lines, length = stacked.shape
+    tile = math.gcd(8, depth)
+    tables = []
+    for table in (blur_y, blur_x.swapaxes(1, 2), blur_x, blur_y.swapaxes(1, 2)):
+        tables.extend(parts_of(table))
+    whole = pl.BlockSpec(padded.shape, lambda v, z: (0, 0, 0))
+    return pl.pallas_call(
+        ratio_kernel,
+        grid=(views, depth // tile),
+        out_shape=jax.ShapeDtypeStruct(padded.shape, jnp.float32),
+        in_specs=[
+            pl.BlockSpec(memory_space=pltpu.SMEM), whole,
+            pl.BlockSpec((None, tile, lines, length), lambda v, z: (v, z, 0, 0)),
+        ] + [pl.BlockSpec((None,) + table.shape[1:], lambda v, z: (v, 0, 0)) for table in tables],
+        out_specs=whole,
+        scratch_shapes=[pltpu.VMEM((tile,) + padded.shape[1:], jnp.float32)],
+        compiler_params=pltpu.CompilerParams(vmem_limit_bytes=40 << 20),
+        cost_estimate=pl.CostEstimate(flops=2 * 10 ** 10, bytes_accessed=1 << 25, transcendentals=0),
+    )(taps_z, padded, stacked, *tables)
+
+
+def swap(axis, place, lower_pair, upper_pair, sems):
+    index, count = lax.axis_index(axis), lax.axis_size(axis)
+    lower = pltpu.make_async_remote_copy(
+        src_ref=lower_pair[0], dst_ref=lower_pair[1], send_sem=sems.at[place, 0], recv_sem=sems.at[place, 1],
+        device_id={axis: index - 1}, device_id_type=MESH,
+    )
+    upper = pltpu.make_async_remote_copy(
+        src_ref=upper_pair[0], dst_ref=upper_pair[1], send_sem=sems.at[place, 2], recv_sem=sems.at[place, 3],
+        device_id={axis: index + 1}, device_id_type=MESH,
+    )
+
+    @pl.when(index > 0)
+    def _():
+        lower.start()
+
+    @pl.when(index < count - 1)
+    def _():
+        upper.start()
+
+    def wait():
+        @pl.when(index > 0)
+        def _():
+            lower.wait_send()
+            upper.wait_recv()
+
+        @pl.when(index == 0)
+        def _():
+            upper_pair[1][...] = jnp.zeros(upper_pair[1].shape, jnp.float32)
+
+        @pl.when(index < count - 1)
+        def _():
+            upper.wait_send()
+            lower.wait_recv()
+
+        @pl.when(index == count - 1)
+        def _():
+            lower_pair[1][...] = jnp.zeros(lower_pair[1].shape, jnp.float32)
+
+    return wait
+
+
+def edges_kernel(width, fold, pad, *refs):
+    refs = list(refs)
+    total = refs.pop(0) if fold else None
+    local = refs.pop(0) if pad else None
+    result = refs.pop(0) if fold else None
+    padded = refs.pop(0) if pad else None
+    from_z, held, to_y, from_y, sems = refs
+    shape = local.shape if pad else result.shape
+    depth, lines = shape[0], shape[1]
+    top, bottom = slice(0, width), slice(lines - width, lines)
+
+    barrier = pltpu.get_barrier_semaphore()
+    for axis in ("view", "pencil"):
+        index, count = lax.axis_index(axis), lax.axis_size(axis)
+        for near, there in ((index - 1, index > 0), (index + 1, index < count - 1)):
+            @pl.when(there)
+            def _(axis=axis, near=near):
+                pl.semaphore_signal(barrier, inc=1, device_id={axis: near}, device_id_type=MESH)
+    peers = 0
+    for axis in ("view", "pencil"):
+        index, count = lax.axis_index(axis), lax.axis_size(axis)
+        peers = peers + jnp.minimum(index, 1) + jnp.minimum(count - 1 - index, 1)
+    pl.semaphore_wait(barrier, peers)
+
+    if fold:
+        wait = swap(
+            "pencil", 0, (total.at[:width], from_z.at[1]),
+            (total.at[depth + width:], from_z.at[0]), sems,
+        )
+
+        @pl.loop(0, depth)
+        def _(z):
+            held[z] = total[width + z]
+
+        wait()
+        for i in range(width):
+            held[i] = held[i] + from_z[0, i]
+            held[depth - width + i] = held[depth - width + i] + from_z[1, i]
+
+        @pl.loop(0, depth)
+        def _(z):
+            to_y[0, 0, z] = held[z, :width]
+            to_y[0, 1, z] = held[z, lines + width:]
+
+        wait = swap(
+            "view", 1, (to_y.at[0, 0], from_y.at[0, 1]), (to_y.at[0, 1], from_y.at[0, 0]), sems,
+        )
+
+        @pl.loop(0, depth)
+        def _(z):
+            result[z] = held[z, width:lines + width]
+
+        wait()
+
+        @pl.loop(0, depth)
+        def _(z):
+            result[z, top] = result[z, top] + from_y[0, 0, z]
+            result[z, bottom] = result[z, bottom] + from_y[0, 1, z]
+            if pad:
+                result[z] = local[z] * result[z] * (1.0 / lax.axis_size("view"))
+
+    if pad:
+        value = result if fold else local
+
+        @pl.loop(0, depth)
+        def _(z):
+            to_y[1, 0, z] = value[z, top]
+            to_y[1, 1, z] = value[z, bottom]
+
+        wait = swap(
+            "view", 2, (to_y.at[1, 0], from_y.at[1, 1]), (to_y.at[1, 1], from_y.at[1, 0]), sems,
+        )
+
+        @pl.loop(0, depth)
+        def _(z):
+            padded[width + z, width:lines + width] = value[z]
+
+        wait()
+
+        @pl.loop(0, depth)
+        def _(z):
+            padded[width + z, :width] = from_y[1, 0, z]
+            padded[width + z, lines + width:] = from_y[1, 1, z]
+
+        wait = swap(
+            "pencil", 3, (padded.at[width:2 * width], padded.at[depth + width:]),
+            (padded.at[depth:depth + width], padded.at[:width]), sems,
+        )
+        wait()
+
+
+def edges(width, number, total=None, local=None):
+    fold, pad = total is not None, local is not None
+    depth, lines, length = local.shape if pad else (total.shape[0] - 2 * width, total.shape[1] - 2 * width, total.shape[2])
+    wide = lines + 2 * width
+    whole, vector = pl.BlockSpec(memory_space=pltpu.VMEM), jnp.float32
+    shapes = []
+    if fold:
+        shapes.append(jax.ShapeDtypeStruct((depth, lines, length), vector))
+    if pad:
+        shapes.append(jax.ShapeDtypeStruct((depth + 2 * width, wide, length), vector))
+    given = [value for value in (total, local) if value is not None]
+    return pl.pallas_call(
+        functools.partial(edges_kernel, width, fold, pad),
+        out_shape=shapes,
+        in_specs=[whole] * len(given),
+        out_specs=[whole] * len(shapes),
+        scratch_shapes=[
+            pltpu.VMEM((2, width, wide, length), vector),
+            pltpu.VMEM((depth, wide, length), vector),
+            pltpu.VMEM((2, 2, depth, width, length), vector),
+            pltpu.VMEM((2, 2, depth, width, length), vector),
+            pltpu.SemaphoreType.DMA((4, 4)),
+        ],
+        compiler_params=pltpu.CompilerParams(
+            collective_id=number, has_side_effects=True, vmem_limit_bytes=24 << 20,
+        ),
+    )(*given)
 
 
 def band(taps, rows, columns, shift):
@@ -283,7 +479,7 @@
     )(sent, recorded, weight, *parts_of(turn), *parts_of(back), picks)
 
 
-def mirrored_weights(weights, half, chunks):
+def mirrored_weights(slab, weights, half, chunks):
     pencils = lax.axis_size("pencil")
     nz, block, _ = weights.shape
     rows = block // chunks
@@ -293,7 +489,7 @@
     flip_z = (positions[:, None] == (nz - positions[None, :]) % nz).astype(jnp.float32)
     flip_x = 0.5 * (lanes[:, None] == half - lanes[None, :]).astype(jnp.float32)
     share = jnp.where(lanes == 0, 1.0, 0.5)
-    result = []
+    sent = []
     for j in range(chunks):
         high = block - j * rows + 1
         if j == 0:
@@ -301,15 +497,17 @@
         else:
             upper = weights[:, high - rows:high, half:]
         facing = mix("zrl,lx->rzx", jnp.flip(upper, axis=1), flip_x)
-        facing = mix("zk,rzx->rkx", flip_z, facing)
-        if j == 0:
-            edge = lax.ppermute(facing[0], "pencil", wrapped)
-        facing = lax.ppermute(facing, "pencil", mirror)
+        sent.append(mix("zk,rzx->rkx", flip_z, facing))
+    slab, *sent = lax.optimization_barrier((slab, *sent))
+    edge = lax.ppermute(sent[0][0], "pencil", wrapped)
+    result = []
+    for j in range(chunks):
+        facing = lax.ppermute(sent[j], "pencil", mirror)
         if j == 0:
             facing = jnp.concatenate([edge[None], facing[1:]], axis=0)
         own = weights[:, j * rows:(j + 1) * rows, :half] * share
         result.append(own.transpose(1, 0, 2) + facing)
-    return jnp.stack(result)
+    return slab, jnp.stack(result)
 
 
 def nyquist_of(slab, weights, half, table_to, turn_z, back_z, table_from):
@@ -338,7 +536,7 @@
     quarter = half // views
     chunks = max(1, block * quarter // 256)
     rows = block // chunks
-    halves = mirrored_weights(weights, half, chunks)
+    slab, halves = mirrored_weights(slab, weights, half, chunks)
 
     to_view = lax.rem(view + jnp.arange(views, dtype=jnp.int32), views)
     source_view = lax.rem(view - jnp.arange(views, dtype=jnp.int32) + views, views)
@@ -392,20 +590,17 @@
     kernels = psf_taps / jnp.sum(psf_taps, axis=-1, keepdims=True)
     margin = kernels.shape[-1] // 2
     depth, rows, length = joined_volume.shape
-    blur_z = band(kernels[:, 0], depth, depth + 2 * margin, 0)
     blur_y = band(kernels[:, 1], rows, rows + 2 * margin, 0)
     blur_x = band(kernels[:, 2], length, length, margin)
     local = 0.1 + jax.nn.softplus(joined_volume)
+    padded, = edges(margin, 1, local=local)
     for repeat in range(ITERS):
-        padded = padded_2(local, (("view", 1), ("pencil", 0)), margin)
-        field = mix("vza,abx->vzbx", blur_z, padded)
-        field = mix("vyb,vzbx->vzyx", blur_y, field)
-        ratio = stacked / mix("vzyx,vcx->vzyc", field, blur_x)
-        field = mix("vzyc,vcx->vzyx", ratio, blur_x)
-        field = mix("vyb,vzyx->vzbx", blur_y, field)
-        total = mix("vza,vzbx->abx", blur_z, field)
-        total = folded(folded(total, "pencil", 0, margin), "view", 1, margin)
-        local = local * total / view_count
+        total = corrections(padded, stacked, kernels[:, 0], blur_y, blur_x)
+        if repeat < ITERS - 1:
+            local, padded = edges(margin, 2, total=total, local=local)
+        else:
+            total, = edges(margin, 3, total=total)
+            local = local * total / view_count
     return (joined_volume, local)
 
 

time: 746 us -> 676 us (0.906)
  Pallas kernels: 236 us -> 376 us
  matrix products: 147 us -> 45.4 us
  waiting for transfers between devices: 151 us -> 81.8 us
  starting transfers between devices: 89.8 us -> 39.8 us
  local copies, waits for them, and re-layouts: 58.2 us -> 68.6 us
    pallas_call x0 -> x5, Pallas kernels: none -> 141 us  [the longest x3 74.2 us: edges(): pl.pallas_call(functools.partial(edges_kernel, width, fold, pad), out_sha...]
    dot_general x28 -> x16, matrix products: 147 us -> 45.4 us  [mix(): return jnp.einsum(form, left, right, precision=lax.Precision.HIGH)]
    ppermute x21 -> x5, starting transfers between devices: 70.5 us -> 20.7 us  [the longest x1 14.5 us: mirrored_weights(): edge = lax.ppermute(sent[0][0], 'pencil', wrapped)]
    ppermute x21 -> x5, waiting for transfers between devices: 38.2 us -> 0.01 us  [the longest x4 0.01 us: mirrored_weights(): facing = lax.ppermute(sent[j], 'pencil', mirror)]
    all_to_all x2, waiting for transfers between devices: 96.9 us -> 81.2 us  [nyquist_of(): lax.all_to_all(line, 'pencil', split_axis=0, concat_axis=0, tiled=True)]
    ppermute x3, waiting for transfers between devices: 16.1 us -> 0.64 us  [exchange(): got.append(lax.ppermute(parts[step], axis, pairs))]
  transfers between devices with their start and end apart: 26 -> 10, of which waited for: 19 -> 3; matrix products, arithmetic and copies ran while one was open for 13% -> 15% of each run, Pallas kernels for 0% -> 0%
where the time goes in v2:
time: 676 us; the launch traced here: 663 us
  Pallas kernels  376 us (56%)
  waiting for transfers between devices  81.8 us (12%)
  local copies, waits for them, and re-layouts  68.6 us (10%)
  other arithmetic  49.1 us (7%)
  matrix products  45.4 us (7%)
  starting transfers between devices  39.8 us (6%)
    pallas_call x1, Pallas kernels, spectral(): pl.pallas_call(functools.partial(spectral_kernel, views, pencils, chunks)...  235 us
    all_to_all x2, waiting for transfers between devices, nyquist_of(): lax.all_to_all(line, 'pencil', split_axis=0, concat_axis=0, tiled=True)  81.2 us
    pallas_call x3, Pallas kernels, edges(): pl.pallas_call(functools.partial(edges_kernel, width, fold, pad), out_sha...  74.2 us
    pallas_call x2, Pallas kernels, corrections(): pl.pallas_call(ratio_kernel, grid=(views, depth // tile), out_shape=jax.S...  66.7 us
    dot_general x16, matrix products, mix(): return jnp.einsum(form, left, right, precision=lax.Precision.HIGH)  45.4 us
    ppermute x1, starting transfers between devices, mirrored_weights(): edge = lax.ppermute(sent[0][0], 'pencil', wrapped)  14.5 us
  transfers between devices with their start and end apart: 10, of which 3 were waited for; matrix products, arithmetic and copies ran while one was open for 15% of the time, Pallas kernels for 0%

profile of v2, /device:TPU:25, one launch (start us, length us, event | category | flops | bytes accessed | tf_op | source)
XLA Modules:
  0.0 663.2 jit_solution(16779806834200554083)
XLA Ops:
  0.7 8.2 %copy.119 = f32[1,256,32,256]{3,1,2,0:T(8,128)S(1)} copy(f32[1,256,32,256]{3,2,1,0:T(8,128)} %param.4) | data formatting | bytes 16777216 | tf_op args[1]
  21.9 14.5 %collective-permute-start = (f32[256,128]{1,0:T(8,128)}, f32[256,128]{1,0:T(8,128)}, u32[]{:S(2)}, u32[]{:S(2)}) collective-permute-start(f32[256,128]{1,0:T(8,128)} %slice_bitcast_fusion), channel_id=1, source_target_pairs={{0,0},{1,7},{2,6},{3,5},{4,4},{5,3},{6,2},{7,1},{8,8},{9,15},{10,1... | collective-permute-start | bytes 393224 | tf_op jit(solution)/shard_map/ppermute | solution.py:502
  41.0 6.4 all-to-all-start
  48.6 3.0 collective-permute-start.3
  64.2 3.3 slice_reduce_fusion
  70.6 3.4 fusion.114
  79.4 4.5 fusion.2
  84.1 9.9 %fusion.15 = f32[2,256,32,128]{3,1,2,0:T(8,128)} fusion(f32[2,128,32,256]{3,1,0,2:T(8,128)S(1)} %fusion.2, f32[1,2,256,256]{3,2,1,0:T(8,128)S(1)} %get-tuple-element.55, f32[1,2,256,256]{3,2,1,0:T(8,128)S(1)} %get-tuple-element.58), kind=kOutput, calls=%fused_computation.21 | convolution fusion | flops 6442713088 | bytes 17825792 | tf_op jit(solution)/shard_map/dcky,zcyx->dkzx/dot_general | solution.py:16
  100.8 11.5 %copy.67 = f32[2,256,32,128]{3,2,1,0:T(8,128)} copy(f32[2,256,32,128]{3,1,2,0:T(8,128)} %fusion.15) | data formatting | bytes 16777216 | tf_op jit(solution)/shard_map/dcky,zcyx->dkzx/dot_general | solution.py:16
  113.7 26.8 %all-to-all-done = f32[8,1,2048]{2,1,0:T(1,128)S(1)} async-done(((f32[8,1,2048]{2,1,0:T(1,128)}), f32[8,1,2048]{2,1,0:T(1,128)S(1)}, u32[]{:S(2)}, u32[]{:S(2)}) %all-to-all-start) | async-done | bytes 65568 | tf_op jit(solution)/shard_map/all_to_all | solution.py:519
  148.7 5.6 all-to-all-start.1
  155.0 54.4 %all-to-all-done.1 = f32[8,1,2048]{2,1,0:T(1,128)S(1)} async-done(((f32[8,1,2048]{2,1,0:T(1,128)}), f32[8,1,2048]{2,1,0:T(1,128)S(1)}, u32[]{:S(2)}, u32[]{:S(2)}) %all-to-all-start.1) | async-done | bytes 65568 | tf_op jit(solution)/shard_map/all_to_all | solution.py:524
  213.1 4.0 fusion.47
  217.1 2.4 pad_maximum_fusion.weight
  219.5 235.4 %shard_map.50 = (f32[4,8,64,256]{3,2,1,0:T(8,128)}, f32[4,32,64,256]{3,2,1,0:T(8,128)}) custom-call(f32[2,8,4,8,32,128]{5,4,3,2,1,0:T(8,128)} %bitcast.219, f32[1,32,256,256]{3,2,1,0:T(8,128)} %recorded.1, f32[4,8,256,128]{3,2,1,0:T(8,128)} %pad_maximum_fusion.weight, bf16[512,512]{1,0:T(8,128)(2,1)} %get-tuple-element.49.turn_high, ...), custom_call_target="tpu_custom_call" | custom-call | flops 10000000000 | bytes 33554432 | tf_op jit(solution)/shard_map/pallas_call | solution.py:455
  454.9 6.1 reshape.778
  461.0 10.7 %fusion.18 = f32[4,32,32,2,64]{4,2,1,0,3:T(8,128)S(1)} fusion(f32[1,1,4,64,8,4,8]{3,6,4,5,1,2,0:T(8,128)S(1)} %copy-done.3, f32[1,1,4,64,8,4,8]{3,6,4,5,1,2,0:T(8,128)S(1)} %copy-done.2, f32[1,1,4,64,8,4,8]{3,6,4,5,1,2,0:T(8,128)S(1)} %copy-done.1, f32[4,8,2,32,8,32]{5,4,3,2,1,0:T(8,128)} %reshape.778), kind=kOutput, calls=%fused_computation.22 | convolution fusion | flops 1611399168 | bytes 4980736 | tf_op jit(solution)/shard_map/jpczrx,dcvypjr->vzxdy/dot_general | solution.py:16
  483.7 4.5 collective-permute-start.6
  512.2 8.0 %fusion.21 = (f32[32,64,256]{2,1,0:T(8,128)S(1)}, f32[32,64,256]{2,1,0:T(8,128)}) fusion(f32[256]{0:T(256)S(1)} %copy-done.46, f32[32,64]{1,0:T(8,128)S(1)} %fusion.183, f32[1,4,32,256]{3,2,1,0:T(8,128)} %get-tuple-element.76, f32[1,4,32,256]{3,2,1,0:T(8,128)} %get-tuple-element.75, f32[1,32,32,2,64]{4,2,1,0,3:T(8,128)} %copy.86, ...), kind=kOutput, calls=%fused_computation.23 | convolution fusion | flops 811663360 | bytes 6562816 | tf_op jit(solution)/shard_map/vzkcy,cvkx->zyx/dot_general | solution.py:16
  520.2 21.8 %shard_map.51.field = f32[40,72,256]{2,1,0:T(8,128)S(1)} custom-call(f32[32,64,256]{2,1,0:T(8,128)S(1)} %get-tuple-element.80.refs_0_.refs_1_), custom_call_target="tpu_custom_call" | custom-call | tf_op jit(solution)/shard_map/pallas_call | solution.py:251
  542.0 33.3 %shard_map.52.refs_0_ = f32[40,72,256]{2,1,0:T(8,128)S(1)} custom-call(f32[4,9]{1,0:T(4,128)S(1)} %get-tuple-element.74.taps, f32[40,72,256]{2,1,0:T(8,128)S(1)} %shard_map.51.field, f32[4,32,64,256]{3,2,1,0:T(8,128)} %get-tuple-element.17.recorded, bf16[4,64,72]{2,1,0:T(8,128)(2,1)S(1)} %get-tuple-element.63.in_high, ...), custom_call_target="tpu_custom_call" | custom-call | flops 20000000000 | bytes 33554432 | tf_op jit(solution)/shard_map/pallas_call | solution.py:93
  575.3 33.7 %shard_map.53 = (f32[32,64,256]{2,1,0:T(8,128)S(1)}, f32[40,72,256]{2,1,0:T(8,128)S(1)}) custom-call(f32[40,72,256]{2,1,0:T(8,128)S(1)} %shard_map.52.refs_0_, f32[32,64,256]{2,1,0:T(8,128)S(1)} %get-tuple-element.80.refs_0_.refs_1_), custom_call_target="tpu_custom_call" | custom-call | tf_op jit(solution)/shard_map/pallas_call | solution.py:251
  609.1 33.3 %shard_map.54.refs_0_ = f32[40,72,256]{2,1,0:T(8,128)S(1)} custom-call(f32[4,9]{1,0:T(4,128)S(1)} %get-tuple-element.74.taps, f32[40,72,256]{2,1,0:T(8,128)S(1)} %get-tuple-element.19.field, f32[4,32,64,256]{3,2,1,0:T(8,128)} %get-tuple-element.17.recorded, bf16[4,64,72]{2,1,0:T(8,128)(2,1)S(1)} %get-tuple-element.63.in_high, ...), custom_call_target="tpu_custom_call" | custom-call | flops 20000000000 | bytes 33554432 | tf_op jit(solution)/shard_map/pallas_call | solution.py:93
  642.4 18.7 %shard_map.55 = f32[32,64,256]{2,1,0:T(8,128)S(1)} custom-call(f32[40,72,256]{2,1,0:T(8,128)S(1)} %shard_map.54.refs_0_), custom_call_target="tpu_custom_call" | custom-call | tf_op jit(solution)/shard_map/pallas_call | solution.py:251
  (242 shorter events, 97.6 us)
Async XLA Ops:
  9.7 28.7 %slice-start = ((s8[8388608]{0:T(1024)(128)(4,1)}), s8[4194304]{0:T(1024)(128)(4,1)S(1)}, s32[]{:S(2)}) async-start(s8[8388608]{0:T(1024)(128)(4,1)} %bitcast.213), calls=%async_computation.2 | async-start | bytes 8388608
  13.4 25.0 %slice-start.1 = ((s8[8388608]{0:T(1024)(128)(4,1)}), s8[4194304]{0:T(1024)(128)(4,1)S(1)}, s32[]{:S(2)}) async-start(s8[8388608]{0:T(1024)(128)(4,1)} %bitcast.213), calls=%async_computation.3 | async-start | bytes 8388608
  19.4 192.4 %collective-permute-start.1 = (f32[8,256,128]{2,1,0:T(8,128)}, f32[8,256,128]{2,1,0:T(8,128)}, u32[]{:S(2)}, u32[]{:S(2)}) collective-permute-start(f32[8,256,128]{2,1,0:T(8,128)} %convolution_bitcast_fusion.7), channel_id=1, source_target_pairs={{0,7},{1,6},{2,5},{3,4},{4,3},{5,2},{6,1},{7,0},{8,15},{9,14},{10,... | collective-permute-start | bytes 3145736 | tf_op jit(solution)/shard_map/ppermute | solution.py:505
  21.9 191.2 %collective-permute-start = (f32[256,128]{1,0:T(8,128)}, f32[256,128]{1,0:T(8,128)}, u32[]{:S(2)}, u32[]{:S(2)}) collective-permute-start(f32[256,128]{1,0:T(8,128)} %slice_bitcast_fusion), channel_id=1, source_target_pairs={{0,0},{1,7},{2,6},{3,5},{4,4},{5,3},{6,2},{7,1},{8,8},{9,15},{10,1... | collective-permute-start | bytes 393224 | tf_op jit(solution)/shard_map/ppermute | solution.py:502
  39.6 28.7 %copy-start.21 = (f32[4,3,9]{2,0,1:T(4,128)S(1)}, f32[4,3,9]{2,0,1:T(4,128)}, u32[]{:S(2)}) copy-start(f32[4,3,9]{2,0,1:T(4,128)} %param.5) | copy-start | bytes 1300
  41.0 99.4 %all-to-all-start = ((f32[8,1,2048]{2,1,0:T(1,128)}), f32[8,1,2048]{2,1,0:T(1,128)S(1)}, u32[]{:S(2)}, u32[]{:S(2)}) async-start(f32[8,1,2048]{2,1,0:T(1,128)} %reshape.827), calls=%async_computation | async-start | bytes 131072 | tf_op jit(solution)/shard_map/all_to_all | solution.py:519
  47.4 165.6 %collective-permute-start.2 = (f32[8,256,128]{2,1,0:T(8,128)}, f32[8,256,128]{2,1,0:T(8,128)}, u32[]{:S(2)}, u32[]{:S(2)}) collective-permute-start(f32[8,256,128]{2,1,0:T(8,128)} %convolution_bitcast_fusion.6), channel_id=1, source_target_pairs={{0,7},{1,6},{2,5},{3,4},{4,3},{5,2},{6,1},{7,0},{8,15},{9,14},{10,... | collective-permute-start | bytes 3145736 | tf_op jit(solution)/shard_map/ppermute | solution.py:505
  48.6 164.4 %collective-permute-start.3 = (f32[8,256,128]{2,1,0:T(8,128)}, f32[8,256,128]{2,1,0:T(8,128)}, u32[]{:S(2)}, u32[]{:S(2)}) collective-permute-start(f32[8,256,128]{2,1,0:T(8,128)} %convolution_bitcast_fusion.5), channel_id=1, source_target_pairs={{0,7},{1,6},{2,5},{3,4},{4,3},{5,2},{6,1},{7,0},{8,15},{9,14},{10,... | collective-permute-start | bytes 3145736 | tf_op jit(solution)/shard_map/ppermute | solution.py:505
  51.6 161.5 %collective-permute-start.4 = (f32[8,256,128]{2,1,0:T(8,128)}, f32[8,256,128]{2,1,0:T(8,128)}, u32[]{:S(2)}, u32[]{:S(2)}) collective-permute-start(f32[8,256,128]{2,1,0:T(8,128)} %convolution_bitcast_fusion.4), channel_id=1, source_target_pairs={{0,7},{1,6},{2,5},{3,4},{4,3},{5,2},{6,1},{7,0},{8,15},{9,14},{10,... | collective-permute-start | bytes 3145736 | tf_op jit(solution)/shard_map/ppermute | solution.py:505
  84.0 13.9 %copy-start.7 = (pred[72,64]{1,0:T(8,128)(4,1)S(1)}, pred[72,64]{1,0:T(8,128)(4,1)}, u32[]{:S(2)}) copy-start(pred[72,64]{1,0:T(8,128)(4,1)} %get-tuple-element.127) | copy-start | bytes 13828
  84.0 13.9 %copy-start.8 = (pred[72,64]{1,0:T(8,128)(4,1)S(1)}, pred[72,64]{1,0:T(8,128)(4,1)}, u32[]{:S(2)}) copy-start(pred[72,64]{1,0:T(8,128)(4,1)} %get-tuple-element.128) | copy-start | bytes 13828
  84.1 13.9 %copy-start.9 = (pred[72,64]{1,0:T(8,128)(4,1)S(1)}, pred[72,64]{1,0:T(8,128)(4,1)}, u32[]{:S(2)}) copy-start(pred[72,64]{1,0:T(8,128)(4,1)} %get-tuple-element.125) | copy-start | bytes 13828
  84.1 13.9 %copy-start.10 = (pred[72,64]{1,0:T(8,128)(4,1)S(1)}, pred[72,64]{1,0:T(8,128)(4,1)}, u32[]{:S(2)}) copy-start(pred[72,64]{1,0:T(8,128)(4,1)} %get-tuple-element.126) | copy-start | bytes 13828
  84.1 13.9 %copy-start.11 = (pred[72,64]{1,0:T(8,128)(4,1)S(1)}, pred[72,64]{1,0:T(8,128)(4,1)}, u32[]{:S(2)}) copy-start(pred[72,64]{1,0:T(8,128)(4,1)} %get-tuple-element.123) | copy-start | bytes 13828
  84.1 13.9 %copy-start.12 = (pred[72,64]{1,0:T(8,128)(4,1)S(1)}, pred[72,64]{1,0:T(8,128)(4,1)}, u32[]{:S(2)}) copy-start(pred[72,64]{1,0:T(8,128)(4,1)} %get-tuple-element.124) | copy-start | bytes 13828
  84.1 13.9 %copy-start.13 = (pred[72,64]{1,0:T(8,128)(4,1)S(1)}, pred[72,64]{1,0:T(8,128)(4,1)}, u32[]{:S(2)}) copy-start(pred[72,64]{1,0:T(8,128)(4,1)} %get-tuple-element.121) | copy-start | bytes 13828
  84.1 13.9 %copy-start.14 = (pred[72,64]{1,0:T(8,128)(4,1)S(1)}, pred[72,64]{1,0:T(8,128)(4,1)}, u32[]{:S(2)}) copy-start(pred[72,64]{1,0:T(8,128)(4,1)} %get-tuple-element.122) | copy-start | bytes 13828
  148.7 60.6 %all-to-all-start.1 = ((f32[8,1,2048]{2,1,0:T(1,128)}), f32[8,1,2048]{2,1,0:T(1,128)S(1)}, u32[]{:S(2)}, u32[]{:S(2)}) async-start(f32[8,1,2048]{2,1,0:T(1,128)} %reshape.829), calls=%async_computation.1 | async-start | bytes 131072 | tf_op jit(solution)/shard_map/all_to_all | solution.py:524
  477.7 17.8 %collective-permute-start.7 = (f32[1040,128]{1,0:T(8,128)}, f32[1040,128]{1,0:T(8,128)}, u32[]{:S(2)}, u32[]{:S(2)}) collective-permute-start(f32[1040,128]{1,0:T(8,128)} %pad_maximum_fusion.10), channel_id=1, source_target_pairs={{0,24},{8,0},{16,8},{24,16},{1,25},{9,1},{17,9},{25,17},{2,26},{10... | collective-permute-start | bytes 1597448 | tf_op jit(solution)/shard_map/ppermute | solution.py:34
  480.4 13.1 %copy-start.4 = (pred[256,256]{1,0:T(8,128)(4,1)S(1)}, pred[256,256]{1,0:T(8,128)(4,1)}, u32[]{:S(2)}) copy-start(pred[256,256]{1,0:T(8,128)(4,1)} %get-tuple-element.111) | copy-start | bytes 196612
  480.4 13.1 %copy-start.5 = (pred[256,256]{1,0:T(8,128)(4,1)S(1)}, pred[256,256]{1,0:T(8,128)(4,1)}, u32[]{:S(2)}) copy-start(pred[256,256]{1,0:T(8,128)(4,1)} %get-tuple-element.112) | copy-start | bytes 196612
  480.4 13.1 %copy-start.25 = (f32[4]{0:T(128)S(1)}, f32[4]{0:T(128)}, u32[]{:S(2)}) copy-start(f32[4]{0:T(128)} %copy-done.24) | copy-start | bytes 52
  483.7 17.3 %collective-permute-start.6 = (f32[1040,128]{1,0:T(8,128)}, f32[1040,128]{1,0:T(8,128)}, u32[]{:S(2)}, u32[]{:S(2)}) collective-permute-start(f32[1040,128]{1,0:T(8,128)} %pad_maximum_fusion.9), channel_id=1, source_target_pairs={{0,16},{8,24},{16,0},{24,8},{1,17},{9,25},{17,1},{25,9},{2,18},{10... | collective-permute-start | bytes 1597448 | tf_op jit(solution)/shard_map/ppermute | solution.py:34
  490.5 16.5 %collective-permute-start.5 = (f32[1040,128]{1,0:T(8,128)}, f32[1040,128]{1,0:T(8,128)}, u32[]{:S(2)}, u32[]{:S(2)}) collective-permute-start(f32[1040,128]{1,0:T(8,128)} %pad_maximum_fusion.8), channel_id=1, source_target_pairs={{0,8},{8,16},{16,24},{24,0},{1,9},{9,17},{17,25},{25,1},{2,10},{10... | collective-permute-start | bytes 1597448 | tf_op jit(solution)/shard_map/ppermute | solution.py:34
  (37 other events, 241.4 us)
